TPU v7x, 128 devices: a whole 4x4x4 slice. The times are simulated.
128 devices in a mesh: model: 16 (over z, y), data: 8 (over x, core).
Axes of the slice: x: 4, y: 4, z: 4, core: 2. Of those that a mesh axis runs over, the one named last changes fastest.
Arguments:
- grad_in: bfloat16 [8, 24, 512, 2048], P('data', None, None, 'model')
- w_in: float32 [24, 512, 2048], P(None, 'data', 'model')
- row_in: float32 [24, 512], P(None, 'data')
- col_in: float32 [24, 2048], P(None, 'model')
- grad_out: bfloat16 [8, 12, 2048, 512], P('data', None, 'model')
- w_out: float32 [12, 2048, 512], P(None, 'model', 'data')
- row_out: float32 [12, 2048], P(None, 'model')
- col_out: float32 [12, 512], P(None, 'data')
- grad_qkv: bfloat16 [8, 54, 512, 512], P('data', None, None, 'model')
- w_qkv: float32 [54, 512, 512], P(None, 'data', 'model')
- row_qkv: float32 [54, 512], P(None, 'data')
- col_qkv: float32 [54, 512], P(None, 'model')
- grad_o: bfloat16 [8, 18, 512, 512], P('data', None, 'model')
- w_o: float32 [18, 512, 512], P(None, 'model', 'data')
- row_o: float32 [18, 512], P(None, 'model')
- col_o: float32 [18, 512], P(None, 'data')
Outputs:
- output 1: float32 [24, 512, 2048], P(None, 'data', 'model')
- output 2: float32 [24, 512], P(None, 'data')
- output 3: float32 [24, 2048], P(None, 'model')
- output 4: float32 [12, 2048, 512], P(None, 'model', 'data')
- output 5: float32 [12, 2048], P(None, 'model')
- output 6: float32 [12, 512], P(None, 'data')
- output 7: float32 [54, 512, 512], P(None, 'data', 'model')
- output 8: float32 [54, 512], P(None, 'data')
- output 9: float32 [54, 512], P(None, 'model')
- output 10: float32 [18, 512, 512], P(None, 'model', 'data')
- output 11: float32 [18, 512], P(None, 'model')
- output 12: float32 [18, 512], P(None, 'data')
All inputs are finite; a program needn't handle non-finite values.
Results may differ from a plain program's by a relative error of at most 0.001.
Values sent between devices are 32-bit elements.
A program may use at most 1 GiB of HBM per device.

v0:
```python
import jax
import jax.numpy as jnp
from jax import lax
from jax.sharding import PartitionSpec as P, NamedSharding

OPT_STEP = 4
EPS_SQ = 1e-30
BETA_TWO = 1.0 - OPT_STEP ** -0.8
LR_BASE = min(1e-2, OPT_STEP ** -0.5)


def finish_update(grad_mean, weight, row_mom, col_mom, row_sum, col_sum, row_axis, full_rows, full_cols):
    new_row = BETA_TWO * row_mom + (1.0 - BETA_TWO) * (row_sum / full_cols)
    new_col = BETA_TWO * col_mom + (1.0 - BETA_TWO) * (col_sum / full_rows)
    row_mean = lax.psum(jnp.sum(new_row, axis=1, keepdims=True), row_axis) / full_rows
    update = grad_mean / jnp.sqrt((new_row / row_mean)[:, :, None] * new_col[:, None, :])
    upd_sq = lax.psum(jnp.sum(update * update, axis=(1, 2), keepdims=True), ('model', 'data'))
    update = update / jnp.maximum(1.0, jnp.sqrt(upd_sq / (full_rows * full_cols)))
    w_sq = lax.psum(jnp.sum(weight * weight, axis=(1, 2), keepdims=True), ('model', 'data'))
    w_rms = jnp.sqrt(w_sq / (full_rows * full_cols))
    return weight - LR_BASE * jnp.maximum(1e-3, w_rms) * update, new_row, new_col


def update_block(grad_parts, weight, row_mom, col_mom, rows_on_data, axis_sizes):
    if rows_on_data:
        row_axis, col_axis, scatter_dim = 'data', 'model', 1
    else:
        row_axis, col_axis, scatter_dim = 'model', 'data', 2
    full_rows = weight.shape[1] * axis_sizes[row_axis]
    full_cols = weight.shape[2] * axis_sizes[col_axis]
    part_sum = lax.psum_scatter(grad_parts[0].astype(jnp.float32), 'data', scatter_dimension=scatter_dim, tiled=True)
    grad_mean = part_sum / axis_sizes['data']
    grad_sq = grad_mean * grad_mean + EPS_SQ
    row_sum = lax.psum(jnp.sum(grad_sq, axis=2), col_axis)
    col_sum = lax.psum(jnp.sum(grad_sq, axis=1), row_axis)
    return finish_update(grad_mean, weight, row_mom, col_mom, row_sum, col_sum, row_axis, full_rows, full_cols)


def solution(mesh):
    axis_sizes = dict(mesh.shape)
    rows_data = (P('data', None, None, 'model'), P(None, 'data', 'model'), P(None, 'data'), P(None, 'model'))
    rows_model = (P('data', None, 'model', None), P(None, 'model', 'data'), P(None, 'model'), P(None, 'data'))

    def step_all(grad_in, w_in, row_in, col_in, grad_out, w_out, row_out, col_out,
                 grad_qkv, w_qkv, row_qkv, col_qkv, grad_o, w_o, row_o, col_o):
        w_in_new, row_in_new, col_in_new = update_block(grad_in, w_in, row_in, col_in, True, axis_sizes)
        w_out_new, row_out_new, col_out_new = update_block(grad_out, w_out, row_out, col_out, False, axis_sizes)
        w_qkv_new, row_qkv_new, col_qkv_new = update_block(grad_qkv, w_qkv, row_qkv, col_qkv, True, axis_sizes)
        w_o_new, row_o_new, col_o_new = update_block(grad_o, w_o, row_o, col_o, False, axis_sizes)
        return (w_in_new, row_in_new, col_in_new, w_out_new, row_out_new, col_out_new,
                w_qkv_new, row_qkv_new, col_qkv_new, w_o_new, row_o_new, col_o_new)

    in_specs = rows_data + rows_model + rows_data + rows_model
    out_specs = rows_data[1:] + rows_model[1:] + rows_data[1:] + rows_model[1:]
    return jax.shard_map(step_all, mesh=mesh, in_specs=in_specs, out_specs=out_specs, check_vma=False)
```

profile of v0, /device:TPU:1, one launch (start us, length us, event | category | flops | bytes accessed | tf_op | source)
XLA Modules:
  0.0 352.0 jit_solution(6361521364936353320)
XLA Ops:
  7.2 1.2 bitcast_convert_fusion.3
  8.4 4.2 %copy.35 = f32[18,32,512]{1,0,2:T(8,128)} copy(f32[18,32,512]{2,1,0:T(8,128)S(1)} %bitcast_convert_fusion.3) | data formatting | bytes 2359296
  12.7 5.1 %reshape.46 = f32[512,576]{1,0:T(8,128)} reshape(f32[512,18,32]{2,1,0:T(8,128)} %bitcast.54) | data formatting | bytes 2359296
  18.8 1.9 bitcast_convert_fusion.2
  20.7 1.9 bitcast_convert_fusion.1
  22.7 8.3 %copy.33 = f32[54,512,32]{2,0,1:T(8,128)} copy(f32[54,512,32]{1,2,0:T(8,128)S(1)} %bitcast_convert_fusion.1) | data formatting | bytes 7077888
  31.0 10.3 %reshape.44 = f32[512,1728]{1,0:T(8,128)} reshape(f32[512,54,32]{2,1,0:T(8,128)} %bitcast.53) | data formatting | bytes 7077888
  41.4 1.8 copy-done.4
  43.2 3.4 bitcast_convert_fusion
  51.0 1.1 reshape.47
  52.5 35.4 %reduce-scatter.11.cloned.1.call-done = f32[12,128,64]{1,2,0:T(8,128)} async-done(((f32[12,128,512]{1,2,0:T(8,128)}), f32[12,128,64]{1,2,0:T(8,128)}) %reduce-scatter.11.cloned.1.call-update) | async-done | bytes 393232 | tf_op jit(solution)/shard_map/reduce_scatter | solution.py:31
  87.9 1.2 fusion.5
  89.1 24.0 %all-reduce.3 = (f32[12,128]{1,0:T(8,128)S(1)}, f32[18,32]{1,0:T(8,128)S(1)}) all-reduce(f32[12,128]{1,0:T(8,128)S(1)} %get-tuple-element.28, f32[18,32]{1,0:T(8,128)S(1)} %get-tuple-element.30), channel_id=1, replica_groups=mesh['model'=16,'data'=8] {'data'}, use_global_device_ids=true, to_apply=%region_15.0 | all-reduce | flops 2112 | bytes 16896 | tf_op jit(solution)/shard_map/psum | solution.py:34
  114.4 11.8 %reduce-scatter.13.cloned.1.call-done = f32[64,1728]{1,0:T(8,128)} async-done(((f32[512,1728]{1,0:T(8,128)}), f32[64,1728]{1,0:T(8,128)}) %reduce-scatter.13.cloned.1.call-update) | async-done | bytes 442384
  126.2 1.7 reshape.45
  128.7 43.7 %reduce-scatter.9.cloned.1.call-done = f32[24,64,128]{2,1,0:T(8,128)} async-done(((f32[24,512,128]{2,1,0:T(8,128)}), f32[24,64,128]{2,1,0:T(8,128)}) %reduce-scatter.9.cloned.1.call-update) | async-done | bytes 786448 | tf_op jit(solution)/shard_map/reduce_scatter | solution.py:31
  172.5 1.5 fusion.3
  174.0 60.8 %all-reduce.1 = (f32[24,64]{1,0:T(8,128)S(1)}, f32[12,64]{1,0:T(8,128)}, f32[12,1]{0,1:T(1,128)S(1)}, f32[54,64]{1,0:T(8,128)S(1)}, f32[18,64]{1,0:T(8,128)S(1)}, /*index=5*/f32[18,1]{0,1:T(1,128)S(1)}) all-reduce(f32[24,64]{1,0:T(8,128)S(1)} %get-tuple-element.26, ...), channel_id=1, replica_groups=mesh['model'=16,'data'=8] {'model'}, use_global_device_ids=true, to_apply=%region_4.0 | all-reduce | flops 6942 | bytes 55536 | tf_op jit(solution)/shard_map/psum | solution.py:34
  235.1 35.8 %all-reduce.2 = (f32[24,128]{1,0:T(8,128)S(1)}, f32[24,1]{0,1:T(1,128)S(1)}, f32[54,32]{1,0:T(8,128)S(1)}, f32[54,1]{0,1:T(1,128)S(1)}) all-reduce(f32[24,128]{1,0:T(8,128)S(1)} %get-tuple-element.27, f32[24,1]{0,1:T(1,128)S(1)} %bitcast.59, f32[54,32]{1,0:T(8,128)S(1)} %get-tuple-element.25, ...), channel_id=1, replica_groups=mesh['model'=16,'data'=8] {'data'}, use_global_device_ids=true, to_apply=%region_8.0 | all-reduce | flops 4878 | bytes 39024 | tf_op jit(solution)/shard_map/psum | solution.py:35
  271.7 1.0 multiply_reduce_fusion
  274.9 64.9 %all-reduce = (f32[24,1,1]{0,2,1:T(1,128)S(1)}, f32[24,1,1]{0,2,1:T(1,128)S(1)}, f32[12,1,1]{0,2,1:T(1,128)S(1)}, f32[12,1,1]{0,2,1:T(1,128)S(1)}, f32[54,1,1]{0...) all-reduce(f32[24,1,1]{0,2,1:T(1,128)S(1)} %bitcast.68, ...), channel_id=1, replica_groups=mesh['model'=16,'data'=8] {'model','data'}, use_global_device_ids=true, to_apply=%region_10.0 | all-reduce | flops 216 | bytes 1728 | tf_op jit(solution)/shard_map/psum | solution.py:17
  339.9 2.0 multiply_subtract_fusion.3
  341.8 1.4 multiply_subtract_fusion
  344.2 1.3 multiply_subtract_fusion.1
  (93 shorter events, 12.3 us)
Async XLA Ops:
  7.2 43.8 %reduce-scatter.15.cloned.1.call-start = ((), (), s32[]{:S(2)}) async-start(), calls=%async_computation.7 | async-start | bytes 1474560
  12.7 5.2 %copy-start.7 = (bf16[1,12,128,512]{3,2,1,0:T(8,128)(2,1)S(1)}, bf16[1,12,128,512]{3,2,1,0:T(8,128)(2,1)}, u32[]{:S(2)}) copy-start(bf16[1,12,128,512]{3,2,1,0:T(8,128)(2,1)} %param.20) | copy-start | bytes 4718596
  17.8 70.2 %reduce-scatter.11.cloned.1.call-start = ((), (), s32[]{:S(2)}) async-start(), calls=%async_computation.5 | async-start | bytes 3538944 | tf_op jit(solution)/shard_map/reduce_scatter | solution.py:31
  20.7 105.5 %reduce-scatter.13.cloned.1.call-start = ((), (), s32[]{:S(2)}) async-start(), calls=%async_computation.6 | async-start | bytes 4128768
  41.3 131.1 %reduce-scatter.9.cloned.1.call-start = ((), (), s32[]{:S(2)}) async-start(), calls=%async_computation.4 | async-start | bytes 7077888 | tf_op jit(solution)/shard_map/reduce_scatter | solution.py:31
  46.6 3.2 copy-start.1
  47.3 65.9 %copy-start.24 = (f32[12,128]{1,0:T(8,128)S(1)}, f32[12,128]{1,0:T(8,128)}, u32[]{:S(2)}) copy-start(f32[12,128]{1,0:T(8,128)} %param.22) | copy-start | bytes 18436
  47.3 66.5 %copy-start.20 = (f32[18,32]{1,0:T(8,128)S(1)}, f32[18,32]{1,0:T(8,128)}, u32[]{:S(2)}) copy-start(f32[18,32]{1,0:T(8,128)} %param.30) | copy-start | bytes 6916
  113.8 159.5 %copy-start.17 = (f32[12,128]{1,0:T(8,128)}, f32[12,128]{1,0:T(8,128)S(1)}, u32[]{:S(2)}) copy-start(f32[12,128]{1,0:T(8,128)S(1)} %get-tuple-element.59) | copy-start | bytes 18436
  114.4 158.4 %copy-start.15 = (f32[18,32]{1,0:T(8,128)}, f32[18,32]{1,0:T(8,128)S(1)}, u32[]{:S(2)}) copy-start(f32[18,32]{1,0:T(8,128)S(1)} %get-tuple-element.57) | copy-start | bytes 6916
  114.4 120.4 %copy-start.18 = (f32[54,64]{1,0:T(8,128)S(1)}, f32[54,64]{1,0:T(8,128)}, u32[]{:S(2)}) copy-start(f32[54,64]{1,0:T(8,128)} %param.26) | copy-start | bytes 41476
  114.4 120.5 %copy-start.21 = (f32[24,64]{1,0:T(8,128)S(1)}, f32[24,64]{1,0:T(8,128)}, u32[]{:S(2)}) copy-start(f32[24,64]{1,0:T(8,128)} %param.18) | copy-start | bytes 18436
  127.9 144.9 %copy-start.22 = (f32[24,128]{1,0:T(8,128)S(1)}, f32[24,128]{1,0:T(8,128)}, u32[]{:S(2)}) copy-start(f32[24,128]{1,0:T(8,128)} %param.19) | copy-start | bytes 36868
  127.9 145.0 %copy-start.23 = (f32[18,64]{1,0:T(8,128)S(1)}, f32[18,64]{1,0:T(8,128)}, u32[]{:S(2)}) copy-start(f32[18,64]{1,0:T(8,128)} %param.31) | copy-start | bytes 13828
  127.9 146.8 %copy-start.3 = (f32[12,128,64]{1,2,0:T(8,128)S(1)}, f32[12,128,64]{1,2,0:T(8,128)}, u32[]{:S(2)}) copy-start(f32[12,128,64]{1,2,0:T(8,128)} %reduce-scatter.11.cloned.1.call-done) | copy-start | bytes 1179652
  128.4 213.4 %copy-start.2 = (f32[54,64,32]{1,2,0:T(8,128)S(1)}, f32[54,64,32]{1,2,0:T(8,128)}, u32[]{:S(2)}) copy-start(f32[54,64,32]{1,2,0:T(8,128)} %param.25) | copy-start | bytes 1327108
  172.5 101.6 %copy-start = (f32[24,64,128]{2,1,0:T(8,128)S(1)}, f32[24,64,128]{2,1,0:T(8,128)}, u32[]{:S(2)}) copy-start(f32[24,64,128]{2,1,0:T(8,128)} %reduce-scatter.9.cloned.1.call-done) | copy-start | bytes 2359300
  234.9 108.3 %copy-start.11 = (f32[54,64]{1,0:T(8,128)}, f32[54,64]{1,0:T(8,128)S(1)}, u32[]{:S(2)}) copy-start(f32[54,64]{1,0:T(8,128)S(1)} %get-tuple-element.53) | copy-start | bytes 41476
  235.1 108.2 %copy-start.16 = (f32[24,64]{1,0:T(8,128)}, f32[24,64]{1,0:T(8,128)S(1)}, u32[]{:S(2)}) copy-start(f32[24,64]{1,0:T(8,128)S(1)} %get-tuple-element.55) | copy-start | bytes 18436
  272.8 71.5 %copy-start.13 = (f32[24,128]{1,0:T(8,128)}, f32[24,128]{1,0:T(8,128)S(1)}, u32[]{:S(2)}) copy-start(f32[24,128]{1,0:T(8,128)S(1)} %multiply_add_fusion.8) | copy-start | bytes 36868
  272.9 71.4 %copy-start.12 = (f32[18,64]{1,0:T(8,128)}, f32[18,64]{1,0:T(8,128)S(1)}, u32[]{:S(2)}) copy-start(f32[18,64]{1,0:T(8,128)S(1)} %multiply_add_fusion.6) | copy-start | bytes 13828
  274.1 71.4 %copy-start.14 = (f32[12,64]{1,0:T(8,128)}, f32[12,64]{1,0:T(8,128)S(1)}, u32[]{:S(2)}) copy-start(f32[12,64]{1,0:T(8,128)S(1)} %multiply_add_fusion.10) | copy-start | bytes 9220
  339.8 3.4 copy-start.9
  339.8 4.4 %copy-start.6 = (f32[24,64,128]{2,1,0:T(8,128)S(1)}, f32[24,64,128]{2,1,0:T(8,128)}, u32[]{:S(2)}) copy-start(f32[24,64,128]{2,1,0:T(8,128)} %param.17) | copy-start | bytes 2359300
  (5 other events, 7.7 us)
Sparse Core Ops, SparseCore 0:
  17.9 33.0 reduce-scatter.14
  53.4 34.4 reduce-scatter.10
  90.4 35.7 reduce-scatter.12
  128.4 43.9 reduce-scatter.8
where the time goes:
time: 353 us; the launch traced here: 352 us
  blocking collectives  186 us (53%)
  waiting for transfers between devices  91.2 us (26%)
  local copies, waits for them, and re-layouts  35.9 us (10%)
  other arithmetic  25.1 us (7%)
  between operations  14 us (4%)
    psum x2, blocking collectives, update_block(): row_sum = lax.psum(jnp.sum(grad_sq, axis=2), col_axis)  84.9 us
    reduce_scatter x2, waiting for transfers between devices, update_block(): lax.psum_scatter(grad_parts[0].astype(jnp.float32), 'data', scatter_dimen...  79.1 us
    psum x1, blocking collectives, finish_update(): lax.psum(jnp.sum(update * update, axis=(1, 2), keepdims=True), ('model',...  64.9 us
    unnamed x61, local copies, waits for them, and re-layouts  35.9 us
    psum x1, blocking collectives, update_block(): col_sum = lax.psum(jnp.sum(grad_sq, axis=1), row_axis)  35.8 us
    unnamed x6, waiting for transfers between devices  12.1 us
    convert_element_type x4, other arithmetic, update_block(): grad_parts[0].astype(jnp.float32)  8.42 us
  transfers between devices with their start and end apart: 4, of which 4 were waited for; matrix products, arithmetic and copies ran while one was open for 10% of the time, Pallas kernels for 0%

commit v1 on v0

v1 whole, which is shorter than its diff:
```python
import functools

import jax
import jax.numpy as jnp
from jax import lax
from jax.experimental import pallas as pl
from jax.experimental.pallas import tpu as pltpu
from jax.sharding import PartitionSpec as P

OPT_STEP = 4
EPS_SQ = 1e-30
BETA_TWO = 1.0 - OPT_STEP ** -0.8
GAIN = 1.0 - BETA_TWO
LR_BASE = min(1e-2, OPT_STEP ** -0.5)
F32 = jnp.float32

N_IN, N_B, N_OUT = 24, 18, 12
N_SUP = N_IN + N_B + N_OUT
FIRST_B, FIRST_OUT = N_IN, N_IN + N_B
ROW_IN, ROW_OUT, ROW_B = 0, 24, 40
CHUNKS = tuple(('in', 6 * i, 6) for i in range(4)) + tuple(('b', FIRST_B + 6 * i, 6) for i in range(3)) \
    + tuple(('out', FIRST_OUT + 6 * i, 6) for i in range(2))
N_CH = len(CHUNKS)
GROUPS = ('in', 'b', 'out')
LAST_CHUNK = {f: max(i for i, c in enumerate(CHUNKS) if c[0] == f) for f in GROUPS}
D2D, OPP_A, OPP_B, OWN_R, OWN_L, MRG_R, MRG_L = range(7)
EX_SLOT = {'in': 0, 'b': 1, 'out': 2, 'w': 3}


def kernel(n_data, n_model, gin_h, gout_h, gq_h, go_h, win_h, wout_h, wq_h, wo_h,
           row_in, col_in, row_out, col_out, sub_b, lane_b, row_o,
           win_o, wout_o, wq_o, wo_o, row_in_o, col_in_o, row_out_o, col_out_o, sub_b_o, lane_b_o,
           gin, gout, gb, part, peer, opp_in, left_in, right_in, grad, wa, wb, w_all, ht,
           lane_sum, rlane, acc_t, comp_b, tab, rsub, wtab, vtab, mod_in, mod_b, mod_out, mod_w,
           scal, dat_in, dat_b, dat_out, got_in, got_b, got_out, got_w, got_s,
           load_sem, w_sem, out_sem, snd, rcv, dsnd, drcv, msnd, mrcv, ssnd, srcv):
    me = lax.axis_index('data')
    mod = lax.axis_index('model')
    n_chips = n_data // 2
    x, c = lax.div(me, 2), lax.rem(me, 2)
    xr, xl, xo = lax.rem(x + 1, n_chips), lax.rem(x + 3, n_chips), lax.rem(x + 2, n_chips)
    partner, right, left = 2 * x + 1 - c, 2 * xr + c, 2 * xl + c
    full = {'in': n_model * 128, 'out': n_model * 128, 'b': n_model * 32}
    count = {'in': N_IN, 'b': N_B, 'out': N_OUT}
    mats = {'in': N_IN, 'b': 4 * N_B, 'out': N_OUT}
    first = {'in': 0, 'b': FIRST_B, 'out': FIRST_OUT}
    row0 = {'in': ROW_IN, 'b': ROW_B, 'out': ROW_OUT}
    mod_blk = {'in': mod_in, 'b': mod_b, 'out': mod_out}
    dat_got = {'in': dat_in, 'b': dat_b, 'out': dat_out}
    mod_got = {'in': got_in, 'b': got_b, 'out': got_out}
    lane_rows = {'in': (0, 24), 'b': (24, 24), 'out': (48, 16)}

    loads = [pltpu.make_async_copy(gin_h.at[pl.ds(6 * i, 6)], gin.at[pl.ds(6 * i, 6)], load_sem.at[i]) for i in range(4)]
    loads.append(pltpu.make_async_copy(gq_h, gb.at[pl.ds(0, 54)], load_sem.at[4]))
    loads.append(pltpu.make_async_copy(go_h, gb.at[pl.ds(54, 18)], load_sem.at[5]))
    loads.append(pltpu.make_async_copy(gout_h, gout, load_sem.at[6]))
    w_loads = [pltpu.make_async_copy(win_h, wa.at[pl.ds(0, 24)], w_sem.at[0]),
               pltpu.make_async_copy(wout_h, wa.at[pl.ds(24, 12)], w_sem.at[1]),
               pltpu.make_async_copy(wq_h, wb.at[pl.ds(0, 54)], w_sem.at[2]),
               pltpu.make_async_copy(wo_h, wb.at[pl.ds(54, 18)], w_sem.at[3])]
    for cp in loads + w_loads:
        cp.start()

    barrier = pltpu.get_barrier_semaphore()

    def hello_data(d, carry):
        pl.semaphore_signal(barrier, inc=1, device_id={'data': lax.rem(me + d, n_data)}, device_id_type=pl.DeviceIdType.MESH)
        return carry

    def hello_model(d, carry):
        pl.semaphore_signal(barrier, inc=1, device_id={'model': lax.rem(mod + d, n_model)}, device_id_type=pl.DeviceIdType.MESH)
        return carry

    lax.fori_loop(1, n_data, hello_data, 0)
    lax.fori_loop(1, n_model, hello_model, 0)

    def remote(src, dst, ssem, rsem, axis, who):
        return pltpu.make_async_remote_copy(src_ref=src, dst_ref=dst, send_sem=ssem, recv_sem=rsem,
                                            device_id={axis: who}, device_id_type=pl.DeviceIdType.MESH)

    def transfer(kind, ch):
        _, b0, n = CHUNKS[ch]
        n_a = n // 2
        every, half_a, half_b = pl.ds(b0, n), pl.ds(b0, n_a), pl.ds(b0 + n_a, n - n_a)
        src, dst, who = {
            D2D: lambda: (part.at[1 - c, :, every], peer.at[:, every], partner),
            OPP_A: lambda: (part.at[c, xo, half_a], opp_in.at[half_a], right),
            OPP_B: lambda: (part.at[c, xo, half_b], opp_in.at[half_b], left),
            OWN_R: lambda: (part.at[c, xr, half_b], left_in.at[half_b], right),
            OWN_L: lambda: (part.at[c, xl, half_a], right_in.at[half_a], left),
            MRG_R: lambda: (part.at[c, xr, half_a], left_in.at[half_a], right),
            MRG_L: lambda: (part.at[c, xl, half_b], right_in.at[half_b], left),
        }[kind]()
        return remote(src, dst, snd.at[kind, ch], rcv.at[kind, ch], 'data', who)

    def convert(ch):
        family, b0, n = CHUNKS[ch]
        if family == 'in':
            loads[ch].wait()
        elif ch == 4:
            loads[4].wait()
            loads[5].wait()
        elif family == 'out' and b0 == FIRST_OUT:
            loads[6].wait()

        def body(i, carry):
            b = b0 + i
            for t in range(n_chips):
                if family == 'in':
                    tile = gin[b, pl.ds(128 * t, 128), :].astype(F32)
                elif family == 'out':
                    tile = gout[b - FIRST_OUT, :, pl.ds(128 * t, 128)].astype(F32).T
                else:
                    four = gb[pl.ds(4 * (b - FIRST_B), 4), :, pl.ds(128 * t, 128)].astype(F32)
                    tile = four.reshape(128, 128).T
                part[0, t, b] = tile[:64]
                part[1, t, b] = tile[64:]
            return carry

        lax.fori_loop(0, n, body, 0)

    def pair(ch):
        _, b0, n = CHUNKS[ch]
        transfer(D2D, ch).wait_recv()

        def add(dest):
            def body(i, carry):
                b = b0 + i
                part[c, dest, b] = part[c, dest, b] + peer[dest, b]
                return carry
            lax.fori_loop(0, n, body, 0)

        add(xo)
        transfer(OPP_A, ch).start()
        transfer(OPP_B, ch).start()
        add(xr)
        transfer(OWN_R, ch).start()
        add(xl)
        transfer(OWN_L, ch).start()
        add(x)

    def merge(ch):
        _, b0, n = CHUNKS[ch]
        n_a = n // 2

        def add(dest, lo, hi):
            def body(b, carry):
                part[c, dest, b] = part[c, dest, b] + opp_in[b]
                return carry
            lax.fori_loop(lo, hi, body, 0)

        transfer(OPP_A, ch).wait_recv()
        add(xr, b0, b0 + n_a)
        transfer(MRG_R, ch).start()
        transfer(OPP_B, ch).wait_recv()
        add(xl, b0 + n_a, b0 + n)
        transfer(MRG_L, ch).start()

    lane_iota = lax.broadcasted_iota(jnp.int32, (64, 128), 1)

    def finish(ch):
        family, b0, n = CHUNKS[ch]
        for kind in (OWN_R, OWN_L, MRG_R, MRG_L):
            transfer(kind, ch).wait_recv()
        base = lane_rows[family][0] - first[family]

        def block(b):
            g = (part[c, x, b] + left_in[b] + right_in[b]) * (1.0 / n_data)
            grad[b] = g
            sq = g * g + EPS_SQ
            lane_sum[pl.ds(base + b, 1), :] = jnp.sum(sq, axis=0, keepdims=True)
            return g, sq

        if family == 'b':
            def body(i, carry):
                b = b0 + i
                g, _ = block(b)
                gt = g.T
                st = (gt * gt + EPS_SQ).reshape(4, 32, 64)
                comp_b[pl.ds(b - FIRST_B, 1), :, 0:64] = jnp.sum(st, axis=1)[None]
                return carry
            lax.fori_loop(0, n, body, 0)
        else:
            which = 0 if family == 'in' else 1

            def body(i, acc):
                b = b0 + i
                _, sq = block(b)
                return jnp.where(lane_iota == b - first[family], jnp.sum(sq, axis=1, keepdims=True), acc)
            acc_t[which] = lax.fori_loop(0, n, body, acc_t[which])

    def gather(src, dst, sems, slot, axis, op):
        send, recv = sems
        rank, n = (me, n_data) if axis == 'data' else (mod, n_model)

        def body(d, carry):
            p = lax.rem(rank + d, n)
            if op == 'start':
                remote(src, dst.at[rank], send.at[slot, p], recv.at[slot, rank], axis, p).start()
            elif op == 'recv':
                remote(src, dst.at[p], send.at[slot, p], recv.at[slot, p], axis, p).wait_recv()
            else:
                remote(src, dst.at[rank], send.at[slot, p], recv.at[slot, rank], axis, p).wait_send()
            return carry

        if op == 'start':
            dst[rank] = src[...]
        lax.fori_loop(1, n, body, 0)

    def total(dst, n):
        acc = dst[0]
        for r in range(1, n):
            acc = acc + dst[r]
        return acc

    d_sems, m_sems, s_sems = (dsnd, drcv), (msnd, mrcv), (ssnd, srcv)

    def lane_ex(family, op):
        r0, n = lane_rows[family]
        gather(lane_sum.at[pl.ds(r0, n)], dat_got[family], d_sems, EX_SLOT[family], 'data', op)

    def model_ex(family, op):
        gather(mod_blk[family], mod_got[family], m_sems, EX_SLOT[family], 'model', op)

    def scal_ex(family, op):
        gather(scal.at[EX_SLOT[family]], got_s.at[EX_SLOT[family]], s_sems, EX_SLOT[family], 'data', op)

    def weights_start():
        for cp in w_loads:
            cp.wait()
        wtab[...] = jnp.zeros_like(wtab)
        vtab[...] = jnp.zeros_like(vtab)

        def body_a(b, carry):
            w = wa[b]
            wtab[pl.ds(b, 1), :] = jnp.sum(w * w, axis=0, keepdims=True)
            return carry

        def body_b(b, carry):
            w = wb[b]
            wtab[pl.ds(ROW_B + b, 1), 0:64] = jnp.sum(w * w, axis=0, keepdims=True)
            return carry

        lax.fori_loop(0, N_IN + N_OUT, body_a, 0)
        lax.fori_loop(0, 4 * N_B, body_b, 0)
        vtab[ROW_OUT:ROW_OUT + N_OUT, :] = row_out[...]
        vtab[ROW_B + 54:ROW_B + 72, 0:32] = row_o[...]
        mod_w[...] = jnp.zeros_like(mod_w)
        mod_w[0:1, :] = jnp.sum(wtab[...].T, axis=0, keepdims=True)
        mod_w[1:2, :] = jnp.sum(vtab[...].T, axis=0, keepdims=True) / n_data
        gather(mod_w, got_w, m_sems, EX_SLOT['w'], 'model', 'start')

    def weights_next():
        gather(mod_w, got_w, m_sems, EX_SLOT['w'], 'model', 'recv')
        scal[EX_SLOT['w']] = total(got_w, n_model)
        scal_ex('w', 'start')

    def weights_done():
        scal_ex('w', 'recv')
        w_all[...] = total(got_s.at[EX_SLOT['w']], n_data)

    def after_lanes(family):
        r0, _ = lane_rows[family]
        n = count[family]
        lane_ex(family, 'recv')
        mom, out = {'in': (col_in, col_in_o), 'out': (row_out, row_out_o), 'b': (lane_b, lane_b_o)}[family]
        new = BETA_TWO * mom[...] + GAIN * (total(dat_got[family], n_data)[:n] / 512.0)
        out[...] = new
        rlane[r0:r0 + n, :] = lax.rsqrt(new)
        if family == 'b':
            def body(s, carry):
                h = grad[FIRST_B + s] * rlane[pl.ds(r0 + s, 1), :]
                t = h.T.reshape(4, 32, 64)
                ht[pl.ds(4 * s, 4)] = t
                comp_b[pl.ds(s, 1), :, 64:128] = jnp.sum(t * t, axis=1)[None]
                return carry
            lax.fori_loop(0, N_B, body, 0)
            mod_b[...] = comp_b[...].reshape(4 * N_B, 128)
        else:
            which = 0 if family == 'in' else 1

            def body(b, acc):
                h = grad[first[family] + b] * rlane[pl.ds(r0 + b, 1), :]
                grad[first[family] + b] = h
                return jnp.where(lane_iota == b, jnp.sum(h * h, axis=1, keepdims=True), acc)
            acc_z = lax.fori_loop(0, n, body, jnp.zeros((64, 128), F32))
            both = jnp.concatenate([acc_t[which], acc_z], axis=0).T
            mod_blk[family][...] = both[:mod_blk[family].shape[0]]
        model_ex(family, 'start')

    def after_model(family):
        n = mats[family]
        model_ex(family, 'recv')
        both = total(mod_got[family], n_model)[:n]
        sums, z = both[:, 0:64], both[:, 64:128]
        mom, out = {'in': (row_in, row_in_o), 'out': (col_out, col_out_o), 'b': (sub_b, sub_b_o)}[family]
        new = BETA_TWO * mom[...] + GAIN * (sums / full[family])
        out[...] = new
        ratio = z / new
        mean_part = GAIN * (sums / 512.0)
        if family == 'in':
            term = new
        elif family == 'out':
            term = mean_part
        else:
            term = jnp.where(lax.broadcasted_iota(jnp.int32, (n, 64), 0) < 54, new, mean_part)
        r0 = row0[family]
        tab[r0:r0 + n, 0:64] = ratio
        tab[r0:r0 + n, 64:128] = term
        turned = tab[...].T
        e = EX_SLOT[family]
        scal[e] = jnp.zeros((8, 128), F32)
        scal[e, 0:1, :] = jnp.sum(turned[:64], axis=0, keepdims=True)
        scal[e, 1:2, :] = jnp.sum(turned[64:], axis=0, keepdims=True)
        scal_ex(family, 'start')
        if family == 'b':
            rsub[e, r0:r0 + n, 0:64] = lax.rsqrt(new)
        else:
            tab[r0:r0 + n, 0:64] = lax.rsqrt(new)
            rsub[e] = tab[...].T

    def after_scalars(family):
        e = EX_SLOT[family]
        scal_ex(family, 'recv')
        tot = total(got_s.at[e], n_data)
        q, s = tot[0:1], tot[1:2]
        w, v = w_all[0:1, :], w_all[1:2, :]
        rows = 512.0 if family == 'in' else float(full[family])
        size = 512.0 * full[family]
        m = (s if family == 'in' else BETA_TWO * v + s) / rows
        scale = jnp.sqrt(m) * (LR_BASE * jnp.maximum(1e-3, jnp.sqrt(w / size))) / jnp.maximum(1.0, jnp.sqrt(m * q / size))
        r0 = row0[family]
        if family == 'b':
            n = mats[family]
            tab[...] = jnp.broadcast_to(scale, (128, 128)).T
            rsub[e, r0:r0 + n, 0:64] = rsub[e, r0:r0 + n, 0:64] * tab[r0:r0 + n, 0:64]

            def body(b, carry):
                wb[b] = wb[b] - ht[b] * rsub[e, pl.ds(r0 + b, 1), 0:64]
                return carry
            lax.fori_loop(0, n, body, 0)
            outs = (pltpu.make_async_copy(wb.at[pl.ds(0, 54)], wq_o, out_sem.at[2]),
                    pltpu.make_async_copy(wb.at[pl.ds(54, 18)], wo_o, out_sem.at[3]))
        else:
            fac = rsub[e, 0:64, :] * scale

            def body(b, carry):
                f = jnp.sum(jnp.where(lane_iota == r0 + b, fac, 0.0), axis=1, keepdims=True)
                wa[r0 + b] = wa[r0 + b] - grad[first[family] + b] * f
                return carry
            lax.fori_loop(0, count[family], body, 0)
            outs = (pltpu.make_async_copy(wa.at[pl.ds(r0, count[family])], win_o if family == 'in' else wout_o,
                                          out_sem.at[0 if family == 'in' else 1]),)
        for cp in outs:
            cp.start()
        return outs

    acc_t[...] = jnp.zeros_like(acc_t)
    tab[...] = jnp.zeros_like(tab)
    lane_sum[...] = jnp.zeros_like(lane_sum)

    convert(0)
    pl.semaphore_wait(barrier, n_data - 1 + n_model - 1)
    pending = []
    for k in range(N_CH + 8):
        if 0 < k < N_CH:
            convert(k)
        if k < N_CH:
            transfer(D2D, k).start()
        if 1 <= k <= N_CH:
            pair(k - 1)
        if 2 <= k <= N_CH + 1:
            merge(k - 2)
        if 3 <= k <= N_CH + 2:
            finish(k - 3)
        if k == 2:
            weights_start()
        if k == 3:
            weights_next()
        if k == 4:
            weights_done()
        for family in GROUPS:
            done = k - (LAST_CHUNK[family] + 3)
            if done == 0:
                lane_ex(family, 'start')
            if done == 1:
                after_lanes(family)
            if done == 2:
                after_model(family)
            if done == 3:
                pending.extend(after_scalars(family))

    for ch in range(N_CH):
        for kind in range(7):
            transfer(kind, ch).wait_send()
    for family in GROUPS:
        lane_ex(family, 'send')
        model_ex(family, 'send')
        scal_ex(family, 'send')
    gather(mod_w, got_w, m_sems, EX_SLOT['w'], 'model', 'send')
    scal_ex('w', 'send')
    for cp in pending:
        cp.wait()


def solution(mesh):
    axis_sizes = dict(mesh.shape)
    n_data, n_model = axis_sizes['data'], axis_sizes['model']
    n_chips = n_data // 2
    rows_data = (P('data', None, None, 'model'), P(None, 'data', 'model'), P(None, 'data'), P(None, 'model'))
    rows_model = (P('data', None, 'model', None), P(None, 'model', 'data'), P(None, 'model'), P(None, 'data'))

    def shape(*dims):
        return jax.ShapeDtypeStruct(dims, F32)

    def vmem(*dims):
        return pltpu.VMEM(dims, F32)

    scratch = [
        pltpu.VMEM((24, 512, 128), jnp.bfloat16), pltpu.VMEM((12, 128, 512), jnp.bfloat16),
        pltpu.VMEM((72, 32, 512), jnp.bfloat16),
        vmem(2, n_chips, N_SUP, 64, 128), vmem(n_chips, N_SUP, 64, 128),
        vmem(N_SUP, 64, 128), vmem(N_SUP, 64, 128), vmem(N_SUP, 64, 128), vmem(N_SUP, 64, 128),
        vmem(36, 64, 128), vmem(72, 32, 64), vmem(8, 128), vmem(72, 32, 64),
        vmem(64, 128), vmem(64, 128), vmem(2, 64, 128), vmem(N_B, 4, 128),
        vmem(128, 128), vmem(3, 128, 128), vmem(128, 128), vmem(128, 128),
        vmem(24, 128), vmem(72, 128), vmem(16, 128), vmem(8, 128),
        vmem(4, 8, 128), vmem(n_data, 24, 128), vmem(n_data, 24, 128), vmem(n_data, 16, 128),
        vmem(n_model, 24, 128), vmem(n_model, 72, 128), vmem(n_model, 16, 128), vmem(n_model, 8, 128),
        vmem(4, n_data, 8, 128),
        pltpu.SemaphoreType.DMA((7,)), pltpu.SemaphoreType.DMA((4,)), pltpu.SemaphoreType.DMA((4,)),
        pltpu.SemaphoreType.DMA((7, N_CH)), pltpu.SemaphoreType.DMA((7, N_CH)),
        pltpu.SemaphoreType.DMA((3, n_data)), pltpu.SemaphoreType.DMA((3, n_data)),
        pltpu.SemaphoreType.DMA((4, n_model)), pltpu.SemaphoreType.DMA((4, n_model)),
        pltpu.SemaphoreType.DMA((4, n_data)), pltpu.SemaphoreType.DMA((4, n_data)),
    ]
    hbm, in_vmem = pl.BlockSpec(memory_space=pl.ANY), pl.BlockSpec(memory_space=pltpu.VMEM)

    def step_all(grad_in, w_in, row_in, col_in, grad_out, w_out, row_out, col_out,
                 grad_qkv, w_qkv, row_qkv, col_qkv, grad_o, w_o, row_o, col_o):
        sub_b = jnp.concatenate([row_qkv, col_o], axis=0)
        lane_b = jnp.concatenate([col_qkv, row_o], axis=0).reshape(N_B, 128)
        outs = pl.pallas_call(
            functools.partial(kernel, n_data, n_model),
            name='adafactor_step',
            out_shape=(shape(24, 64, 128), shape(12, 64, 128), shape(54, 32, 64), shape(18, 32, 64),
                       shape(24, 64), shape(24, 128), shape(12, 128), shape(12, 64), shape(72, 64), shape(N_B, 128)),
            in_specs=[hbm] * 8 + [in_vmem] * 7,
            out_specs=[hbm] * 4 + [in_vmem] * 6,
            scratch_shapes=scratch,
            compiler_params=pltpu.CompilerParams(collective_id=0, has_side_effects=True, vmem_limit_bytes=60 * 1024 * 1024),
        )(grad_in[0], grad_out[0], grad_qkv[0].transpose(0, 2, 1), grad_o[0],
          w_in, w_out.transpose(0, 2, 1), w_qkv.transpose(0, 2, 1), w_o,
          row_in, col_in, row_out, col_out, sub_b, lane_b, row_o)
        w_in_new, w_out_new, w_qkv_new, w_o_new, row_in_new, col_in_new, row_out_new, col_out_new, sub_new, lane_new = outs
        lane_new = lane_new.reshape(72, 32)
        return (w_in_new, row_in_new, col_in_new, w_out_new.transpose(0, 2, 1), row_out_new, col_out_new,
                w_qkv_new.transpose(0, 2, 1), sub_new[:54], lane_new[:54], w_o_new, lane_new[54:], sub_new[54:])

    in_specs = rows_data + rows_model + rows_data + rows_model
    out_specs = rows_data[1:] + rows_model[1:] + rows_data[1:] + rows_model[1:]
    return jax.shard_map(step_all, mesh=mesh, in_specs=in_specs, out_specs=out_specs, check_vma=False)
```

time: 353 us -> 124 us (0.35)
  blocking collectives: 186 us -> 0 us
  Pallas kernels: 0 us -> 107 us
  waiting for transfers between devices: 91.2 us -> 0 us
  other arithmetic: 25.1 us -> 2.18 us
  local copies, waits for them, and re-layouts: 35.9 us -> 13.3 us
  between operations: 14 us -> 0.71 us
    psum x4 -> x0, blocking collectives: 186 us -> none  [the longest x2 84.9 us: update_block(): row_sum = lax.psum(jnp.sum(grad_sq, axis=2), col_axis)]
    pallas_call x0 -> x1, Pallas kernels: none -> 107 us  [step_all(): pl.pallas_call(functools.partial(kernel, n_data, n_model), name='adafacto...]
    reduce_scatter x2 -> x0, waiting for transfers between devices: 79.1 us -> none  [update_block(): lax.psum_scatter(grad_parts[0].astype(jnp.float32), 'data', scatter_dimen...]
    unnamed x61 -> x24, local copies, waits for them, and re-layouts: 35.9 us -> 8.4 us
    unnamed x6 -> x0, waiting for transfers between devices: 12.1 us -> none
    reduce_sum x16 -> x0, other arithmetic: 10 us -> none  [the longest x4 3.19 us: finish_update(): jnp.sum(weight * weight, axis=(1, 2), keepdims=True)]
    convert_element_type x4 -> x0, other arithmetic: 8.42 us -> none  [update_block(): grad_parts[0].astype(jnp.float32)]
    sub x4 -> x0, other arithmetic: 5.58 us -> none  [finish_update(): weight - LR_BASE * jnp.maximum(0.001, w_rms) * update]
  transfers between devices with their start and end apart: 4 -> 0, of which waited for: 4 -> 0; matrix products, arithmetic and copies ran while one was open for 10% -> 0% of each run, Pallas kernels for 0% -> 0%
where the time goes in v1:
time: 124 us; the launch traced here: 123 us
  Pallas kernels  107 us (86%)
  local copies, waits for them, and re-layouts  13.3 us (11%)
  other arithmetic  2.18 us (2%)
    pallas_call x1, Pallas kernels, step_all(): pl.pallas_call(functools.partial(kernel, n_data, n_model), name='adafacto...  107 us
    unnamed x24, local copies, waits for them, and re-layouts  8.4 us

profile of v1, /device:TPU:1, one launch (start us, length us, event | category | flops | bytes accessed | tf_op | source)
XLA Modules:
  0.0 123.5 jit_solution(7277365098884372208)
XLA Ops:
  0.6 1.4 %pad_maximum_fusion.sub_b = f32[72,64]{1,0:T(8,128)} fusion(f32[18,64]{1,0:T(8,128)} %param.31, f32[54,64]{1,0:T(8,128)} %param.26), kind=kLoop, calls=%fused_computation | loop fusion | flops 4608 | bytes 36864 | tf_op jit(solution)/shard_map/concatenate | solution.py:441
  2.0 0.8 copy.31
  2.8 0.8 pad_maximum_fusion.1
  3.6 0.1 copy.32
  3.7 0.7 reshape.30.lane_b
  4.4 107.3 %adafactor_step.1 = (f32[24,64,128]{2,1,0:T(8,128)}, f32[12,64,128]{2,1,0:T(8,128)}, f32[54,32,64]{2,1,0:T(8,128)}, f32[18,32,64]{2,1,0:T(8,128)}, f32[24,64]{1,...) custom-call(bf16[24,512,128]{2,1,0:T(8,128)(2,1)} %bitcast.10, ...), custom_call_target="tpu_custom_call" | custom-call | tf_op jit(solution)/shard_map/adafactor_step/pallas_call | solution.py:443
  111.6 0.0 copy-start.4
  111.7 0.0 copy-start.3
  111.7 0.0 copy-start.1
  111.7 0.0 copy-start.6
  111.7 0.0 copy-start.5
  111.7 1.5 %slice.12 = f32[54,64]{1,0:T(8,128)} slice(f32[72,64]{1,0:T(8,128)} %get-tuple-element.29), slice={[0:54], [0:64]} | slice | bytes 27648 | tf_op jit(solution)/shard_map/slice | solution.py:458
  113.2 0.8 reshape.31
  113.9 0.7 copy.33
  114.6 0.6 slice.17
  115.2 1.3 %slice.15 = f32[18,64]{1,0:T(8,128)} slice(f32[72,64]{1,0:T(8,128)} %get-tuple-element.29), slice={[54:72], [0:64]} | slice | bytes 9216 | tf_op jit(solution)/shard_map/slice | solution.py:458
  116.6 2.1 %copy.42 = f32[24,64,128]{2,1,0:T(8,128)} copy(f32[24,64,128]{2,1,0:T(8,128)} %get-tuple-element.68) | data formatting | bytes 1572864
  118.7 0.6 copy.43
  119.3 0.6 copy.44
  119.9 0.7 copy.45
  120.6 0.6 copy.46
  121.2 0.6 copy.47
  121.8 0.9 copy.48
  122.8 0.7 copy.49
  (10 shorter events, 0.0 us)
Async XLA Ops:
  111.6 7.0 %copy-start.4 = (f32[24,64]{1,0:T(8,128)S(1)}, f32[24,64]{1,0:T(8,128)}, u32[]{:S(2)}) copy-start(f32[24,64]{1,0:T(8,128)} %get-tuple-element.69) | copy-start | bytes 18436
  111.7 7.6 %copy-start.3 = (f32[24,128]{1,0:T(8,128)S(1)}, f32[24,128]{1,0:T(8,128)}, u32[]{:S(2)}) copy-start(f32[24,128]{1,0:T(8,128)} %get-tuple-element.70) | copy-start | bytes 36868
  111.7 8.2 %copy-start.1 = (f32[12,64,128]{2,1,0:T(8,128)S(1)}, f32[12,64,128]{2,1,0:T(8,128)}, u32[]{:S(2)}) copy-start(f32[12,64,128]{2,1,0:T(8,128)} %get-tuple-element.25) | copy-start | bytes 1179652
  111.7 9.0 %copy-start.6 = (f32[12,128]{1,0:T(8,128)S(1)}, f32[12,128]{1,0:T(8,128)}, u32[]{:S(2)}) copy-start(f32[12,128]{1,0:T(8,128)} %get-tuple-element.72) | copy-start | bytes 18436
  111.7 9.6 %copy-start.5 = (f32[12,64]{1,0:T(8,128)S(1)}, f32[12,64]{1,0:T(8,128)}, u32[]{:S(2)}) copy-start(f32[12,64]{1,0:T(8,128)} %get-tuple-element.73) | copy-start | bytes 9220
  111.7 10.1 %copy-start = (f32[54,32,64]{2,1,0:T(8,128)S(1)}, f32[54,32,64]{2,1,0:T(8,128)}, u32[]{:S(2)}) copy-start(f32[54,32,64]{2,1,0:T(8,128)} %get-tuple-element.28) | copy-start | bytes 1327108
  116.5 6.2 %copy-start.2 = (f32[18,32,64]{2,1,0:T(8,128)S(1)}, f32[18,32,64]{2,1,0:T(8,128)}, u32[]{:S(2)}) copy-start(f32[18,32,64]{2,1,0:T(8,128)} %get-tuple-element.77) | copy-start | bytes 442372

commit v2 on v1

v2 whole, which is shorter than its diff:
```python
import functools

import jax
import jax.numpy as jnp
from jax import lax
from jax.experimental import pallas as pl
from jax.experimental.pallas import tpu as pltpu
from jax.sharding import PartitionSpec as P

OPT_STEP = 4
EPS_SQ = 1e-30
BETA_TWO = 1.0 - OPT_STEP ** -0.8
GAIN = 1.0 - BETA_TWO
LR_BASE = min(1e-2, OPT_STEP ** -0.5)
F32 = jnp.float32
LANES, ROWS, WIDE = 128, 64, 32
VMEM_LIMIT = 60 * 10 ** 6

N_IN, N_B, N_OUT = 24, 18, 12
N_SUP = N_IN + N_B + N_OUT
FIRST_B, FIRST_IN, FIRST_OUT = 0, N_B, N_B + N_IN
N_QKV, N_O = 54, 18
ROW_IN, ROW_OUT, ROW_B = 0, 24, 40
SIZES = (('b', (2, 4, 6, 6)), ('in', (6, 6, 6, 6)), ('out', (6, 4, 2)))


def cut():
    chunks, at = [], 0
    for family, sizes in SIZES:
        for n in sizes:
            chunks.append((family, at, n))
            at += n
    return tuple(chunks)


CHUNKS = cut()
N_CH = len(CHUNKS)
GROUPS = ('out', 'in', 'b')
LAST_CHUNK = {f: max(i for i, c in enumerate(CHUNKS) if c[0] == f) for f in GROUPS}
D2D, OPP_A, OPP_B, OWN_R, OWN_L, MRG_R, MRG_L = range(7)
EX_SLOT = {'in': 0, 'b': 1, 'out': 2, 'w': 3}
AHEAD, EARLY_OWN, LAG_MERGE, LAG_FINISH = 2, 3, 2, 3
LAG_STATS = {'b': (1, 3, 5), 'in': (1, 3, 4), 'out': (1, 2, 3)}


def kernel(n_data, n_model, gin_h, gout_h, gq_h, go_h, win_h, wout_h, wq_h, wo_h,
           row_in_h, col_in_h, row_out_h, col_out_h, row_q_h, col_q_h, row_o_h, col_o_h,
           w_in, w_out, w_q, w_o, row_in_o, col_in_o, row_out_o, col_out_o, row_q_o, col_q_o, row_o_o, col_o_o,
           row_in, col_in, row_out, col_out, row_q, col_q, row_o, col_o, lane_b, turn,
           gin, gout, gb, part, peer, opp_in, left_in, right_in, grad, w_all, ht,
           lane_sum, rlane, acc_t, comp_b, tab, rsub, wtab, vtab, mod_in, mod_b, mod_out, mod_w,
           scal, dat_in, dat_b, dat_out, got_in, got_b, got_out, got_w, got_s,
           load_sem, w_sem, small_sem, snd, rcv, dsnd, drcv, msnd, mrcv, ssnd, srcv):
    me = lax.axis_index('data')
    mod = lax.axis_index('model')
    n_chips = n_data // 2
    x, c = lax.div(me, 2), lax.rem(me, 2)
    xr, xl, xo = lax.rem(x + 1, n_chips), lax.rem(x + 3, n_chips), lax.rem(x + 2, n_chips)
    partner, right, left = 2 * x + 1 - c, 2 * xr + c, 2 * xl + c
    full = {'in': n_model * LANES, 'out': n_model * LANES, 'b': n_model * WIDE}
    count = {'in': N_IN, 'b': N_B, 'out': N_OUT}
    mats = {'in': N_IN, 'b': 4 * N_B, 'out': N_OUT}
    first = {'in': FIRST_IN, 'b': FIRST_B, 'out': FIRST_OUT}
    row0 = {'in': ROW_IN, 'b': ROW_B, 'out': ROW_OUT}
    mod_blk = {'in': mod_in, 'b': mod_b, 'out': mod_out}
    dat_got = {'in': dat_in, 'b': dat_b, 'out': dat_out}
    mod_got = {'in': got_in, 'b': got_b, 'out': got_out}
    lane_rows = {'in': (0, 24), 'b': (24, 24), 'out': (48, 16)}

    loads = [pltpu.make_async_copy(gq_h.at[pl.ds(0, 8)], gb.at[pl.ds(0, 8)], load_sem.at[0]),
             pltpu.make_async_copy(gq_h.at[pl.ds(8, 46)], gb.at[pl.ds(8, 46)], load_sem.at[1]),
             pltpu.make_async_copy(go_h, gb.at[pl.ds(54, 18)], load_sem.at[2]),
             pltpu.make_async_copy(gin_h, gin, load_sem.at[3]),
             pltpu.make_async_copy(gout_h, gout, load_sem.at[4])]
    w_loads = [pltpu.make_async_copy(win_h, w_in, w_sem.at[0]),
               pltpu.make_async_copy(wout_h, w_out, w_sem.at[1]),
               pltpu.make_async_copy(wq_h, w_q, w_sem.at[2]),
               pltpu.make_async_copy(wo_h, w_o, w_sem.at[3])]
    small = [pltpu.make_async_copy(src, dst, small_sem.at[i]) for i, (src, dst) in enumerate((
        (row_in_h, row_in), (col_in_h, col_in), (row_out_h, row_out), (col_out_h, col_out),
        (row_q_h, row_q), (col_q_h, col_q), (row_o_h, row_o), (col_o_h, col_o)))]
    for cp in loads:
        cp.start()

    barrier = pltpu.get_barrier_semaphore()

    def hello_data(d, carry):
        pl.semaphore_signal(barrier, inc=1, device_id={'data': lax.rem(me + d, n_data)}, device_id_type=pl.DeviceIdType.MESH)
        return carry

    def hello_model(d, carry):
        pl.semaphore_signal(barrier, inc=1, device_id={'model': lax.rem(mod + d, n_model)}, device_id_type=pl.DeviceIdType.MESH)
        return carry

    lax.fori_loop(1, n_data, hello_data, 0)
    lax.fori_loop(1, n_model, hello_model, 0)

    def remote(src, dst, ssem, rsem, axis, who):
        return pltpu.make_async_remote_copy(src_ref=src, dst_ref=dst, send_sem=ssem, recv_sem=rsem,
                                            device_id={axis: who}, device_id_type=pl.DeviceIdType.MESH)

    def transfer(kind, ch):
        _, b0, n = CHUNKS[ch]
        n_a = n // 2
        every, half_a, half_b = pl.ds(b0, n), pl.ds(b0, n_a), pl.ds(b0 + n_a, n - n_a)
        src, dst, who = {
            D2D: lambda: (part.at[1 - c, :, every], peer.at[:, every], partner),
            OPP_A: lambda: (part.at[c, xo, half_a], opp_in.at[half_a], right),
            OPP_B: lambda: (part.at[c, xo, half_b], opp_in.at[half_b], left),
            OWN_R: lambda: (part.at[c, xr, half_b], left_in.at[half_b], right),
            OWN_L: lambda: (part.at[c, xl, half_a], right_in.at[half_a], left),
            MRG_R: lambda: (part.at[c, xr, half_a], left_in.at[half_a], right),
            MRG_L: lambda: (part.at[c, xl, half_b], right_in.at[half_b], left),
        }[kind]()
        return remote(src, dst, snd.at[kind, ch], rcv.at[kind, ch], 'data', who)

    def convert(ch):
        family, b0, n = CHUNKS[ch]
        if ch == 0:
            loads[0].wait()
        elif ch == 1:
            loads[1].wait()
            loads[2].wait()
        elif b0 == FIRST_IN:
            loads[3].wait()
        elif b0 == FIRST_OUT:
            loads[4].wait()

        def body(i, carry):
            b = b0 + i
            for t in range(n_chips):
                if family == 'in':
                    tile = gin[b - FIRST_IN, pl.ds(LANES * t, LANES), :].astype(F32)
                elif family == 'out':
                    tile = gout[b - FIRST_OUT, :, pl.ds(LANES * t, LANES)].astype(F32).T
                else:
                    four = gb[pl.ds(4 * (b - FIRST_B), 4), :, pl.ds(LANES * t, LANES)].astype(F32)
                    tile = four.reshape(LANES, LANES).T
                part[0, t, b] = tile[:ROWS]
                part[1, t, b] = tile[ROWS:]
            return carry

        lax.fori_loop(0, n, body, 0)

    def add_peer(ch, dest):
        _, b0, n = CHUNKS[ch]

        def body(i, carry):
            b = b0 + i
            part[c, dest, b] = part[c, dest, b] + peer[dest, b]
            return carry
        lax.fori_loop(0, n, body, 0, unroll=2)

    def opposite(ch):
        transfer(D2D, ch).wait_recv()
        add_peer(ch, xo)
        transfer(OPP_A, ch).start()
        transfer(OPP_B, ch).start()
        add_peer(ch, xr)
        add_peer(ch, xl)
        if ch < EARLY_OWN:
            own(ch)
        add_peer(ch, x)

    def own(ch):
        transfer(OWN_R, ch).start()
        transfer(OWN_L, ch).start()

    def merge(ch):
        _, b0, n = CHUNKS[ch]
        n_a = n // 2

        def add(dest, lo, hi):
            def body(b, carry):
                part[c, dest, b] = part[c, dest, b] + opp_in[b]
                return carry
            lax.fori_loop(lo, hi, body, 0)

        transfer(OPP_A, ch).wait_recv()
        add(xr, b0, b0 + n_a)
        transfer(MRG_R, ch).start()
        transfer(OPP_B, ch).wait_recv()
        add(xl, b0 + n_a, b0 + n)
        transfer(MRG_L, ch).start()
        if ch >= EARLY_OWN:
            own(ch)

    lane_iota = lax.broadcasted_iota(jnp.int32, (ROWS, LANES), 1)

    def finish(ch):
        family, b0, n = CHUNKS[ch]
        for kind in (OWN_R, OWN_L, MRG_R, MRG_L):
            transfer(kind, ch).wait_recv()
        base = lane_rows[family][0] - first[family]

        def block(b):
            g = (part[c, x, b] + left_in[b] + right_in[b]) * (1.0 / n_data)
            grad[b] = g
            sq = g * g + EPS_SQ
            lane_sum[pl.ds(base + b, 1), :] = jnp.sum(sq, axis=0, keepdims=True)
            return g, sq

        if family == 'b':
            def body(i, carry):
                b = b0 + i
                g, _ = block(b)
                gt = g.T
                st = (gt * gt + EPS_SQ).reshape(4, WIDE, ROWS)
                comp_b[pl.ds(b - FIRST_B, 1), :, 0:ROWS] = jnp.sum(st, axis=1)[None]
                return carry
            lax.fori_loop(0, n, body, 0, unroll=2)
        else:
            which = 0 if family == 'in' else 1

            def body(i, acc):
                b = b0 + i
                _, sq = block(b)
                return jnp.where(lane_iota == b - first[family], jnp.sum(sq, axis=1, keepdims=True), acc)
            acc_t[which] = lax.fori_loop(0, n, body, acc_t[which], unroll=2)

    def gather(src, dst, sems, slot, axis, op):
        send, recv = sems
        rank, n = (me, n_data) if axis == 'data' else (mod, n_model)

        def body(d, carry):
            p = lax.rem(rank + d, n)
            if op == 'start':
                remote(src, dst.at[rank], send.at[slot, p], recv.at[slot, rank], axis, p).start()
            elif op == 'recv':
                remote(src, dst.at[p], send.at[slot, p], recv.at[slot, p], axis, p).wait_recv()
            else:
                remote(src, dst.at[rank], send.at[slot, p], recv.at[slot, rank], axis, p).wait_send()
            return carry

        if op == 'start':
            dst[rank] = src[...]
        lax.fori_loop(1, n, body, 0)

    def total(dst, n):
        acc = dst[0]
        for r in range(1, n):
            acc = acc + dst[r]
        return acc

    d_sems, m_sems, s_sems = (dsnd, drcv), (msnd, mrcv), (ssnd, srcv)

    def lane_ex(family, op):
        r0, n = lane_rows[family]
        gather(lane_sum.at[pl.ds(r0, n)], dat_got[family], d_sems, EX_SLOT[family], 'data', op)

    def model_ex(family, op):
        gather(mod_blk[family], mod_got[family], m_sems, EX_SLOT[family], 'model', op)

    def scal_ex(family, op):
        gather(scal.at[EX_SLOT[family]], got_s.at[EX_SLOT[family]], s_sems, EX_SLOT[family], 'data', op)

    def weights_start():
        for cp in w_loads + small:
            cp.wait()
        turn[...] = jnp.zeros_like(turn)
        turn[0:WIDE, 0:N_QKV] = col_q[...]
        turn[...] = turn[...].T
        turn[N_QKV:N_QKV + N_O, 0:WIDE] = row_o[...]
        row = turn[pl.ds(0, N_B, stride=4), :]
        for q in range(1, 4):
            row = row + pltpu.roll(turn[pl.ds(q, N_B, stride=4), :], WIDE * q, 1)
        lane_b[...] = row
        wtab[...] = jnp.zeros_like(wtab)
        vtab[...] = jnp.zeros_like(vtab)

        def squares(ref, row, width):
            def body(b, carry):
                w = ref[b]
                wtab[pl.ds(row + b, 1), 0:width] = jnp.sum(w * w, axis=0, keepdims=True)
                return carry
            lax.fori_loop(0, ref.shape[0], body, 0, unroll=6)

        squares(w_in, ROW_IN, LANES)
        squares(w_out, ROW_OUT, LANES)
        squares(w_q, ROW_B, ROWS)
        squares(w_o, ROW_B + N_QKV, ROWS)
        vtab[ROW_OUT:ROW_OUT + N_OUT, :] = row_out[...]
        vtab[ROW_B + 54:ROW_B + 72, 0:WIDE] = row_o[...]
        mod_w[...] = jnp.zeros_like(mod_w)
        mod_w[0:1, :] = jnp.sum(wtab[...].T, axis=0, keepdims=True)
        mod_w[1:2, :] = jnp.sum(vtab[...].T, axis=0, keepdims=True) / n_data
        gather(mod_w, got_w, m_sems, EX_SLOT['w'], 'model', 'start')

    def weights_next():
        gather(mod_w, got_w, m_sems, EX_SLOT['w'], 'model', 'recv')
        scal[EX_SLOT['w']] = total(got_w, n_model)
        scal_ex('w', 'start')

    def weights_done():
        scal_ex('w', 'recv')
        w_all[...] = total(got_s.at[EX_SLOT['w']], n_data)

    def after_lanes(family):
        r0, _ = lane_rows[family]
        n = count[family]
        lane_ex(family, 'recv')
        mom, out = {'in': (col_in, col_in_o), 'out': (row_out, row_out_o), 'b': (lane_b, None)}[family]
        new = BETA_TWO * mom[...] + GAIN * (total(dat_got[family], n_data)[:n] / 512.0)
        rlane[r0:r0 + n, :] = lax.rsqrt(new)
        if family == 'b':
            def body(s, carry):
                h = grad[FIRST_B + s] * rlane[pl.ds(r0 + s, 1), :]
                t = h.T.reshape(4, WIDE, ROWS)
                ht[pl.ds(4 * s, 4)] = t
                comp_b[pl.ds(s, 1), :, ROWS:LANES] = jnp.sum(t * t, axis=1)[None]
                return carry
            lax.fori_loop(0, N_B, body, 0, unroll=3)
            mod_b[...] = comp_b[...].reshape(4 * N_B, LANES)
        else:
            which = 0 if family == 'in' else 1

            def body(b, acc):
                h = grad[first[family] + b] * rlane[pl.ds(r0 + b, 1), :]
                grad[first[family] + b] = h
                return jnp.where(lane_iota == b, jnp.sum(h * h, axis=1, keepdims=True), acc)
            acc_z = lax.fori_loop(0, n, body, jnp.zeros((ROWS, LANES), F32), unroll=4)
            both = jnp.concatenate([acc_t[which], acc_z], axis=0).T
            mod_blk[family][...] = both[:mod_blk[family].shape[0]]
        model_ex(family, 'start')
        if family == 'b':
            turn[...] = jnp.zeros_like(turn)
            for q in range(4):
                turn[pl.ds(q, N_B, stride=4), :] = pltpu.roll(new, (LANES - WIDE * q) % LANES, 1)
            row_o_o[...] = turn[N_QKV:N_QKV + N_O, 0:WIDE]
            turn[...] = turn[...].T
            col_q_o[...] = turn[0:WIDE, 0:N_QKV]
        else:
            out[...] = new

    def after_model(family):
        n = mats[family]
        model_ex(family, 'recv')
        both = total(mod_got[family], n_model)[:n]
        sums, z = both[:, 0:ROWS], both[:, ROWS:LANES]
        if family == 'b':
            mom = jnp.concatenate([row_q[...], col_o[...]], axis=0)
        else:
            mom = (row_in if family == 'in' else col_out)[...]
        new = BETA_TWO * mom + GAIN * (sums / full[family])
        ratio = z / new
        mean_part = GAIN * (sums / 512.0)
        if family == 'in':
            term = new
        elif family == 'out':
            term = mean_part
        else:
            term = jnp.where(lax.broadcasted_iota(jnp.int32, (n, ROWS), 0) < 54, new, mean_part)
        r0 = row0[family]
        tab[r0:r0 + n, 0:ROWS] = ratio
        tab[r0:r0 + n, ROWS:LANES] = term
        turned = tab[...].T
        e = EX_SLOT[family]
        scal[e] = jnp.zeros((8, LANES), F32)
        scal[e, 0:1, :] = jnp.sum(turned[:ROWS], axis=0, keepdims=True)
        scal[e, 1:2, :] = jnp.sum(turned[ROWS:], axis=0, keepdims=True)
        scal_ex(family, 'start')
        if family == 'b':
            row_q_o[...] = new[:N_QKV]
            col_o_o[...] = new[N_QKV:]
            rsub[e, r0:r0 + n, 0:ROWS] = lax.rsqrt(new)
        else:
            (row_in_o if family == 'in' else col_out_o)[...] = new
            tab[r0:r0 + n, 0:ROWS] = lax.rsqrt(new)
            rsub[e] = tab[...].T

    def after_scalars(family):
        e = EX_SLOT[family]
        scal_ex(family, 'recv')
        tot = total(got_s.at[e], n_data)
        q, s = tot[0:1], tot[1:2]
        w, v = w_all[0:1, :], w_all[1:2, :]
        rows = 512.0 if family == 'in' else float(full[family])
        size = 512.0 * full[family]
        m = (s if family == 'in' else BETA_TWO * v + s) / rows
        scale = jnp.sqrt(m) * (LR_BASE * jnp.maximum(1e-3, jnp.sqrt(w / size))) / jnp.maximum(1.0, jnp.sqrt(m * q / size))
        r0 = row0[family]
        if family == 'b':
            n = mats[family]
            tab[...] = jnp.broadcast_to(scale, (LANES, LANES)).T
            rsub[e, r0:r0 + n, 0:ROWS] = rsub[e, r0:r0 + n, 0:ROWS] * tab[r0:r0 + n, 0:ROWS]

            for ref, b0 in ((w_q, 0), (w_o, N_QKV)):
                def body(b, carry, ref=ref, b0=b0):
                    ref[b] = ref[b] - ht[b0 + b] * rsub[e, pl.ds(r0 + b0 + b, 1), 0:ROWS]
                    return carry
                lax.fori_loop(0, ref.shape[0], body, 0, unroll=6)
        else:
            ref = w_in if family == 'in' else w_out
            fac = rsub[e, 0:ROWS, :] * scale

            def body(b, carry):
                f = jnp.sum(jnp.where(lane_iota == r0 + b, fac, 0.0), axis=1, keepdims=True)
                ref[b] = ref[b] - grad[first[family] + b] * f
                return carry
            lax.fori_loop(0, count[family], body, 0, unroll=4)

    def sent_early():
        for ch in range(N_CH):
            for kind in range(7):
                transfer(kind, ch).wait_send()
        gather(mod_w, got_w, m_sems, EX_SLOT['w'], 'model', 'send')
        scal_ex('w', 'send')
        for family in ('b', 'in'):
            lane_ex(family, 'send')
            model_ex(family, 'send')
            scal_ex(family, 'send')

    def sent_late():
        lane_ex('out', 'send')
        model_ex('out', 'send')
        scal_ex('out', 'send')

    acc_t[...] = jnp.zeros_like(acc_t)
    tab[...] = jnp.zeros_like(tab)
    lane_sum[...] = jnp.zeros_like(lane_sum)

    convert(0)
    for cp in small + w_loads:
        cp.start()
    pl.semaphore_wait(barrier, n_data - 1 + n_model - 1)
    transfer(D2D, 0).start()
    last = N_CH - 1 + LAG_FINISH
    for k in range(1 - AHEAD, last + 1 + LAG_STATS['out'][2]):
        if k + AHEAD < N_CH:
            convert(k + AHEAD)
            transfer(D2D, k + AHEAD).start()
        if 0 <= k < N_CH:
            opposite(k)
        if 0 <= k - LAG_MERGE < N_CH:
            merge(k - LAG_MERGE)
        if 0 <= k - LAG_FINISH < N_CH:
            finish(k - LAG_FINISH)
        if k == 4:
            weights_start()
        if k == 5:
            weights_next()
        if k == 6:
            weights_done()
        for family in GROUPS:
            after = k - (LAST_CHUNK[family] + LAG_FINISH)
            if after == 0:
                lane_ex(family, 'start')
            if after == LAG_STATS[family][0]:
                after_lanes(family)
            if after == LAG_STATS[family][1]:
                after_model(family)
            if after == LAG_STATS[family][2]:
                after_scalars(family)
        if k == last + 1:
            sent_early()
    sent_late()


def deliver(*refs):
    srcs, dsts, sem = refs[:12], refs[12:24], refs[24]
    copies = [pltpu.make_async_copy(src, dst, sem.at[i]) for i, (src, dst) in enumerate(zip(srcs, dsts))]
    for cp in copies:
        cp.start()
    for cp in copies:
        cp.wait()


def solution(mesh):
    axis_sizes = dict(mesh.shape)
    n_data, n_model = axis_sizes['data'], axis_sizes['model']
    n_chips = n_data // 2
    rows_data = (P('data', None, None, 'model'), P(None, 'data', 'model'), P(None, 'data'), P(None, 'model'))
    rows_model = (P('data', None, 'model', None), P(None, 'model', 'data'), P(None, 'model'), P(None, 'data'))

    def vmem(*dims):
        return pltpu.VMEM(dims, F32)

    small = (vmem(24, ROWS), vmem(24, LANES), vmem(12, LANES), vmem(12, ROWS), vmem(54, ROWS), vmem(WIDE, 54), vmem(18, WIDE), vmem(18, ROWS))
    results = (vmem(24, ROWS, LANES), vmem(12, ROWS, LANES), vmem(54, WIDE, ROWS), vmem(18, WIDE, ROWS), *small)
    scratch = [
        *small, vmem(N_B, LANES), vmem(LANES, LANES),
        pltpu.VMEM((24, 512, LANES), jnp.bfloat16), pltpu.VMEM((12, LANES, 512), jnp.bfloat16),
        pltpu.VMEM((72, WIDE, 512), jnp.bfloat16),
        vmem(2, n_chips, N_SUP, ROWS, LANES), vmem(n_chips, N_SUP, ROWS, LANES),
        vmem(N_SUP, ROWS, LANES), vmem(N_SUP, ROWS, LANES), vmem(N_SUP, ROWS, LANES), vmem(N_SUP, ROWS, LANES),
        vmem(8, LANES), vmem(72, WIDE, ROWS),
        vmem(ROWS, LANES), vmem(ROWS, LANES), vmem(2, ROWS, LANES), vmem(N_B, 4, LANES),
        vmem(LANES, LANES), vmem(3, LANES, LANES), vmem(LANES, LANES), vmem(LANES, LANES),
        vmem(24, LANES), vmem(72, LANES), vmem(16, LANES), vmem(8, LANES),
        vmem(4, 8, LANES), vmem(n_data, 24, LANES), vmem(n_data, 24, LANES), vmem(n_data, 16, LANES),
        vmem(n_model, 24, LANES), vmem(n_model, 72, LANES), vmem(n_model, 16, LANES), vmem(n_model, 8, LANES),
        vmem(4, n_data, 8, LANES),
        pltpu.SemaphoreType.DMA((5,)), pltpu.SemaphoreType.DMA((4,)), pltpu.SemaphoreType.DMA((8,)),
        pltpu.SemaphoreType.DMA((7, N_CH)), pltpu.SemaphoreType.DMA((7, N_CH)),
        pltpu.SemaphoreType.DMA((3, n_data)), pltpu.SemaphoreType.DMA((3, n_data)),
        pltpu.SemaphoreType.DMA((4, n_model)), pltpu.SemaphoreType.DMA((4, n_model)),
        pltpu.SemaphoreType.DMA((4, n_data)), pltpu.SemaphoreType.DMA((4, n_data)),
    ]
    hbm, in_vmem = pl.BlockSpec(memory_space=pltpu.HBM), pl.BlockSpec(memory_space=pltpu.VMEM)

    def step_all(grad_in, w_in, row_in, col_in, grad_out, w_out, row_out, col_out,
                 grad_qkv, w_qkv, row_qkv, col_qkv, grad_o, w_o, row_o, col_o):
        kept = pl.pallas_call(
            functools.partial(kernel, n_data, n_model),
            name='adafactor_step',
            out_shape=results,
            in_specs=[hbm] * 16,
            out_specs=[in_vmem] * 12,
            scratch_shapes=scratch,
            compiler_params=pltpu.CompilerParams(collective_id=0, has_side_effects=True, vmem_limit_bytes=VMEM_LIMIT),
        )(grad_in[0], grad_out[0], grad_qkv[0].transpose(0, 2, 1), grad_o[0],
          w_in, w_out.transpose(0, 2, 1), w_qkv.transpose(0, 2, 1), w_o,
          row_in, col_in, row_out, col_out, row_qkv, col_qkv.T, row_o, col_o)
        (w_in_new, w_out_new, w_qkv_new, w_o_new, row_in_new, col_in_new, row_out_new, col_out_new,
         row_qkv_new, col_qkv_new, row_o_new, col_o_new) = pl.pallas_call(
            deliver,
            name='deliver',
            out_shape=[jax.ShapeDtypeStruct(r.shape, F32) for r in results],
            in_specs=[in_vmem] * 12,
            out_specs=[hbm] * 12,
            scratch_shapes=[pltpu.SemaphoreType.DMA((12,))],
            compiler_params=pltpu.CompilerParams(vmem_limit_bytes=10 ** 6),
        )(*(pltpu.with_memory_space_constraint(a, pltpu.VMEM) for a in kept))
        return (w_in_new, row_in_new, col_in_new, w_out_new.transpose(0, 2, 1), row_out_new, col_out_new,
                w_qkv_new.transpose(0, 2, 1), row_qkv_new, col_qkv_new.T, w_o_new, row_o_new, col_o_new)

    in_specs = rows_data + rows_model + rows_data + rows_model
    out_specs = rows_data[1:] + rows_model[1:] + rows_data[1:] + rows_model[1:]
    return jax.shard_map(step_all, mesh=mesh, in_specs=in_specs, out_specs=out_specs, check_vma=False)
```

time: 124 us -> 93 us (0.75)
  Pallas kernels: 107 us -> 92.2 us
  local copies, waits for them, and re-layouts: 13.3 us -> 0 us
  other arithmetic: 2.18 us -> 0 us
    pallas_call x1, Pallas kernels: 107 us -> 90.7 us  [step_all(): pl.pallas_call(functools.partial(kernel, n_data, n_model), name='adafacto...]
    unnamed x24 -> x0, local copies, waits for them, and re-layouts: 8.4 us -> none
    slice x4 -> x0, local copies, waits for them, and re-layouts: 3.37 us -> none  [the longest x1 1.46 us: step_all(): sub_new[:54]]
    concatenate x2 -> x0, other arithmetic: 2.18 us -> none  [the longest x1 1.39 us: step_all(): sub_b = jnp.concatenate([row_qkv, col_o], axis=0)]
    pallas_call x0 -> x1, Pallas kernels: none -> 1.53 us  [step_all(): pl.pallas_call(deliver, name='deliver', out_shape=[jax.ShapeDtypeStruct(r...]
    reshape x2 -> x0, local copies, waits for them, and re-layouts: 1.46 us -> none  [the longest x1 0.78 us: step_all(): lane_new = lane_new.reshape(72, 32)]
where the time goes in v2:
time: 93 us; the launch traced here: 92.9 us
  Pallas kernels  92.2 us (99%)
    pallas_call x1, Pallas kernels, step_all(): pl.pallas_call(functools.partial(kernel, n_data, n_model), name='adafacto...  90.7 us

profile of v2, /device:TPU:1, one launch (start us, length us, event | category | flops | bytes accessed | tf_op | source)
XLA Modules:
  0.0 92.9 jit_solution(6449650129688146645)
XLA Ops:
  0.7 90.7 %adafactor_step.1 = (f32[24,64,128]{2,1,0:T(8,128)S(1)}, f32[12,64,128]{2,1,0:T(8,128)S(1)}, f32[54,32,64]{2,1,0:T(8,128)S(1)}, f32[18,32,64]{2,1,0:T(8,128)S(1)...) custom-call(bf16[24,512,128]{2,1,0:T(8,128)(2,1)} %bitcast.12, ...), custom_call_target="tpu_custom_call" | custom-call | tf_op jit(solution)/shard_map/adafactor_step/pallas_call | solution.py:503
  91.3 1.5 %deliver.1 = (f32[24,64,128]{2,1,0:T(8,128)}, f32[12,64,128]{2,1,0:T(8,128)}, f32[54,32,64]{2,1,0:T(8,128)}, f32[18,32,64]{2,1,0:T(8,128)}, f32[24,64]{1,0:T(8,1...) custom-call(f32[24,64,128]{2,1,0:T(8,128)S(1)} %get-tuple-element.36, ...), custom_call_target="tpu_custom_call" | custom-call | tf_op jit(solution)/shard_map/deliver/pallas_call | solution.py:515

commit v3 on v2

--- a/solution.py
+++ b/solution.py
@@ -35,12 +35,15 @@
 
 CHUNKS = cut()
 N_CH = len(CHUNKS)
-GROUPS = ('out', 'in', 'b')
+GROUPS = ('b', 'in', 'out')
 LAST_CHUNK = {f: max(i for i, c in enumerate(CHUNKS) if c[0] == f) for f in GROUPS}
 D2D, OPP_A, OPP_B, OWN_R, OWN_L, MRG_R, MRG_L = range(7)
+SEND = (0, 1, 1, 2, 3, 2, 3)
+LEFT, RIGHT = 3, 4
+RECV = (D2D, OPP_A, OPP_B, LEFT, RIGHT, LEFT, RIGHT)
 EX_SLOT = {'in': 0, 'b': 1, 'out': 2, 'w': 3}
 AHEAD, EARLY_OWN, LAG_MERGE, LAG_FINISH = 2, 3, 2, 3
-LAG_STATS = {'b': (1, 3, 5), 'in': (1, 3, 4), 'out': (1, 2, 3)}
+LAG_STATS = {'b': (1, 3, 5), 'in': (1, 4, 5), 'out': (1, 2, 3)}
 
 
 def kernel(n_data, n_model, gin_h, gout_h, gq_h, go_h, win_h, wout_h, wq_h, wo_h,
@@ -84,16 +87,21 @@
 
     barrier = pltpu.get_barrier_semaphore()
 
-    def hello_data(d, carry):
-        pl.semaphore_signal(barrier, inc=1, device_id={'data': lax.rem(me + d, n_data)}, device_id_type=pl.DeviceIdType.MESH)
-        return carry
-
-    def hello_model(d, carry):
-        pl.semaphore_signal(barrier, inc=1, device_id={'model': lax.rem(mod + d, n_model)}, device_id_type=pl.DeviceIdType.MESH)
-        return carry
-
-    lax.fori_loop(1, n_data, hello_data, 0)
-    lax.fori_loop(1, n_model, hello_model, 0)
+    def others(axis):
+        side = 2 if axis == 'data' else 4
+        n, rank = (n_data, me) if axis == 'data' else (n_model, mod)
+        high, low, rows = lax.div(rank, side), lax.rem(rank, side), n // side
+
+        def hops(d):
+            up, over = d // side, d % side
+            return min(up, rows - up) * (side - 1) + min(over, side - over)
+
+        for d in sorted(range(1, n), key=lambda d: -hops(d)):
+            yield lax.rem(high + d // side, rows) * side + lax.rem(low + d % side, side)
+
+    for axis in ('model', 'data'):
+        for who in others(axis):
+            pl.semaphore_signal(barrier, inc=1, device_id={axis: who}, device_id_type=pl.DeviceIdType.MESH)
 
     def remote(src, dst, ssem, rsem, axis, who):
         return pltpu.make_async_remote_copy(src_ref=src, dst_ref=dst, send_sem=ssem, recv_sem=rsem,
@@ -112,7 +120,7 @@
             MRG_R: lambda: (part.at[c, xr, half_a], left_in.at[half_a], right),
             MRG_L: lambda: (part.at[c, xl, half_b], right_in.at[half_b], left),
         }[kind]()
-        return remote(src, dst, snd.at[kind, ch], rcv.at[kind, ch], 'data', who)
+        return remote(src, dst, snd.at[SEND[kind]], rcv.at[RECV[kind], ch], 'data', who)
 
     def convert(ch):
         family, b0, n = CHUNKS[ch]
@@ -189,8 +197,9 @@
 
     def finish(ch):
         family, b0, n = CHUNKS[ch]
-        for kind in (OWN_R, OWN_L, MRG_R, MRG_L):
-            transfer(kind, ch).wait_recv()
+        every = pl.ds(b0, n)
+        remote(left_in.at[every], left_in.at[every], snd.at[2], rcv.at[LEFT, ch], 'data', right).wait_recv()
+        remote(right_in.at[every], right_in.at[every], snd.at[3], rcv.at[RIGHT, ch], 'data', left).wait_recv()
         base = lane_rows[family][0] - first[family]
 
         def block(b):
@@ -219,22 +228,19 @@
             acc_t[which] = lax.fori_loop(0, n, body, acc_t[which], unroll=2)
 
     def gather(src, dst, sems, slot, axis, op):
-        send, recv = sems
+        send, recv = sems[0].at[slot], sems[1].at[slot]
         rank, n = (me, n_data) if axis == 'data' else (mod, n_model)
-
-        def body(d, carry):
-            p = lax.rem(rank + d, n)
-            if op == 'start':
-                remote(src, dst.at[rank], send.at[slot, p], recv.at[slot, rank], axis, p).start()
-            elif op == 'recv':
-                remote(src, dst.at[p], send.at[slot, p], recv.at[slot, p], axis, p).wait_recv()
-            else:
-                remote(src, dst.at[rank], send.at[slot, p], recv.at[slot, rank], axis, p).wait_send()
-            return carry
-
         if op == 'start':
             dst[rank] = src[...]
-        lax.fori_loop(1, n, body, 0)
+            for who in others(axis):
+                remote(src, dst.at[rank], send, recv, axis, who).start()
+            return
+        rest = dst.at[pl.ds(0, n - 1)]
+        done = remote(rest, rest, send, recv, axis, rank)
+        if op == 'recv':
+            done.wait_recv()
+        else:
+            done.wait_send()
 
     def total(dst, n):
         acc = dst[0]
@@ -281,7 +287,6 @@
         squares(w_o, ROW_B + N_QKV, ROWS)
         vtab[ROW_OUT:ROW_OUT + N_OUT, :] = row_out[...]
         vtab[ROW_B + 54:ROW_B + 72, 0:WIDE] = row_o[...]
-        mod_w[...] = jnp.zeros_like(mod_w)
         mod_w[0:1, :] = jnp.sum(wtab[...].T, axis=0, keepdims=True)
         mod_w[1:2, :] = jnp.sum(vtab[...].T, axis=0, keepdims=True) / n_data
         gather(mod_w, got_w, m_sems, EX_SLOT['w'], 'model', 'start')
@@ -355,7 +360,6 @@
         tab[r0:r0 + n, ROWS:LANES] = term
         turned = tab[...].T
         e = EX_SLOT[family]
-        scal[e] = jnp.zeros((8, LANES), F32)
         scal[e, 0:1, :] = jnp.sum(turned[:ROWS], axis=0, keepdims=True)
         scal[e, 1:2, :] = jnp.sum(turned[ROWS:], axis=0, keepdims=True)
         scal_ex(family, 'start')
@@ -400,9 +404,8 @@
             lax.fori_loop(0, count[family], body, 0, unroll=4)
 
     def sent_early():
-        for ch in range(N_CH):
-            for kind in range(7):
-                transfer(kind, ch).wait_send()
+        for i, ref in enumerate((peer, opp_in, left_in, right_in)):
+            remote(ref, ref, snd.at[i], rcv.at[0, 0], 'data', partner).wait_send()
         gather(mod_w, got_w, m_sems, EX_SLOT['w'], 'model', 'send')
         scal_ex('w', 'send')
         for family in ('b', 'in'):
@@ -426,33 +429,35 @@
     transfer(D2D, 0).start()
     last = N_CH - 1 + LAG_FINISH
     for k in range(1 - AHEAD, last + 1 + LAG_STATS['out'][2]):
+        if 0 <= k < N_CH:
+            opposite(k)
         if k + AHEAD < N_CH:
             convert(k + AHEAD)
             transfer(D2D, k + AHEAD).start()
-        if 0 <= k < N_CH:
-            opposite(k)
-        if 0 <= k - LAG_MERGE < N_CH:
-            merge(k - LAG_MERGE)
-        if 0 <= k - LAG_FINISH < N_CH:
-            finish(k - LAG_FINISH)
+        for ch in range(N_CH):
+            if k == ch + (LAG_MERGE if ch < N_CH - 1 else 1):
+                merge(ch)
         if k == 4:
             weights_start()
-        if k == 5:
+        if k == 6:
             weights_next()
-        if k == 6:
+        if k == 8:
             weights_done()
+        if k == last + 2:
+            sent_early()
         for family in GROUPS:
             after = k - (LAST_CHUNK[family] + LAG_FINISH)
-            if after == 0:
-                lane_ex(family, 'start')
             if after == LAG_STATS[family][0]:
                 after_lanes(family)
             if after == LAG_STATS[family][1]:
                 after_model(family)
             if after == LAG_STATS[family][2]:
                 after_scalars(family)
-        if k == last + 1:
-            sent_early()
+        if 0 <= k - LAG_FINISH < N_CH:
+            finish(k - LAG_FINISH)
+        for family in GROUPS:
+            if k == LAST_CHUNK[family] + LAG_FINISH:
+                lane_ex(family, 'start')
     sent_late()
 
 
@@ -483,18 +488,16 @@
         pltpu.VMEM((72, WIDE, 512), jnp.bfloat16),
         vmem(2, n_chips, N_SUP, ROWS, LANES), vmem(n_chips, N_SUP, ROWS, LANES),
         vmem(N_SUP, ROWS, LANES), vmem(N_SUP, ROWS, LANES), vmem(N_SUP, ROWS, LANES), vmem(N_SUP, ROWS, LANES),
-        vmem(8, LANES), vmem(72, WIDE, ROWS),
+        vmem(2, LANES), vmem(72, WIDE, ROWS),
         vmem(ROWS, LANES), vmem(ROWS, LANES), vmem(2, ROWS, LANES), vmem(N_B, 4, LANES),
         vmem(LANES, LANES), vmem(3, LANES, LANES), vmem(LANES, LANES), vmem(LANES, LANES),
-        vmem(24, LANES), vmem(72, LANES), vmem(16, LANES), vmem(8, LANES),
-        vmem(4, 8, LANES), vmem(n_data, 24, LANES), vmem(n_data, 24, LANES), vmem(n_data, 16, LANES),
-        vmem(n_model, 24, LANES), vmem(n_model, 72, LANES), vmem(n_model, 16, LANES), vmem(n_model, 8, LANES),
-        vmem(4, n_data, 8, LANES),
+        vmem(24, LANES), vmem(72, LANES), vmem(16, LANES), vmem(2, LANES),
+        vmem(4, 2, LANES), vmem(n_data, 24, LANES), vmem(n_data, 24, LANES), vmem(n_data, 16, LANES),
+        vmem(n_model, 24, LANES), vmem(n_model, 72, LANES), vmem(n_model, 16, LANES), vmem(n_model, 2, LANES),
+        vmem(4, n_data, 2, LANES),
         pltpu.SemaphoreType.DMA((5,)), pltpu.SemaphoreType.DMA((4,)), pltpu.SemaphoreType.DMA((8,)),
-        pltpu.SemaphoreType.DMA((7, N_CH)), pltpu.SemaphoreType.DMA((7, N_CH)),
-        pltpu.SemaphoreType.DMA((3, n_data)), pltpu.SemaphoreType.DMA((3, n_data)),
-        pltpu.SemaphoreType.DMA((4, n_model)), pltpu.SemaphoreType.DMA((4, n_model)),
-        pltpu.SemaphoreType.DMA((4, n_data)), pltpu.SemaphoreType.DMA((4, n_data)),
+        pltpu.SemaphoreType.DMA((4,)), pltpu.SemaphoreType.DMA((5, N_CH)),
+        *(pltpu.SemaphoreType.DMA((n,)) for n in (3, 3, 4, 4, 4, 4)),
     ]
     hbm, in_vmem = pl.BlockSpec(memory_space=pltpu.HBM), pl.BlockSpec(memory_space=pltpu.VMEM)
 

time: 93 us -> 86.7 us (0.932)
  Pallas kernels: 92.2 us -> 85.9 us
    pallas_call x1, Pallas kernels: 90.7 us -> 84.4 us  [step_all(): pl.pallas_call(functools.partial(kernel, n_data, n_model), name='adafacto...]
where the time goes in v3:
time: 86.7 us; the launch traced here: 86.6 us
  Pallas kernels  85.9 us (99%)
    pallas_call x1, Pallas kernels, step_all(): pl.pallas_call(functools.partial(kernel, n_data, n_model), name='adafacto...  84.4 us

profile of v3, /device:TPU:1, one launch (start us, length us, event | category | flops | bytes accessed | tf_op | source)
XLA Modules:
  0.0 86.6 jit_solution(5965878336215534390)
XLA Ops:
  0.7 84.4 %adafactor_step.1 = (f32[24,64,128]{2,1,0:T(8,128)S(1)}, f32[12,64,128]{2,1,0:T(8,128)S(1)}, f32[54,32,64]{2,1,0:T(8,128)S(1)}, f32[18,32,64]{2,1,0:T(8,128)S(1)...) custom-call(bf16[24,512,128]{2,1,0:T(8,128)(2,1)} %bitcast.12, ...), custom_call_target="tpu_custom_call" | custom-call | tf_op jit(solution)/shard_map/adafactor_step/pallas_call | solution.py:506
  85.0 1.5 %deliver.1 = (f32[24,64,128]{2,1,0:T(8,128)}, f32[12,64,128]{2,1,0:T(8,128)}, f32[54,32,64]{2,1,0:T(8,128)}, f32[18,32,64]{2,1,0:T(8,128)}, f32[24,64]{1,0:T(8,1...) custom-call(f32[24,64,128]{2,1,0:T(8,128)S(1)} %get-tuple-element.36, ...), custom_call_target="tpu_custom_call" | custom-call | tf_op jit(solution)/shard_map/deliver/pallas_call | solution.py:518

commit v4 on v3

--- a/solution.py
+++ b/solution.py
@@ -21,29 +21,30 @@
 FIRST_B, FIRST_IN, FIRST_OUT = 0, N_B, N_B + N_IN
 N_QKV, N_O = 54, 18
 ROW_IN, ROW_OUT, ROW_B = 0, 24, 40
-SIZES = (('b', (2, 4, 6, 6)), ('in', (6, 6, 6, 6)), ('out', (6, 4, 2)))
+GROUPS = {'b': ('b', FIRST_B, N_B), 'in': ('in', FIRST_IN, N_IN), 'out_a': ('out', FIRST_OUT, 8), 'out_b': ('out', FIRST_OUT + 8, 4)}
+SIZES = (('b', (2, 4, 6, 6)), ('in', (6, 6, 6, 6)), ('out_a', (4, 4)), ('out_b', (2, 2)))
 
 
 def cut():
     chunks, at = [], 0
-    for family, sizes in SIZES:
+    for group, sizes in SIZES:
         for n in sizes:
-            chunks.append((family, at, n))
+            chunks.append((group, at, n))
             at += n
     return tuple(chunks)
 
 
 CHUNKS = cut()
 N_CH = len(CHUNKS)
-GROUPS = ('b', 'in', 'out')
-LAST_CHUNK = {f: max(i for i, c in enumerate(CHUNKS) if c[0] == f) for f in GROUPS}
+LAST_CHUNK = {g: max(i for i, c in enumerate(CHUNKS) if c[0] == g) for g in GROUPS}
 D2D, OPP_A, OPP_B, OWN_R, OWN_L, MRG_R, MRG_L = range(7)
 SEND = (0, 1, 1, 2, 3, 2, 3)
 LEFT, RIGHT = 3, 4
 RECV = (D2D, OPP_A, OPP_B, LEFT, RIGHT, LEFT, RIGHT)
-EX_SLOT = {'in': 0, 'b': 1, 'out': 2, 'w': 3}
+SLOT = {'b': 0, 'in': 1, 'out_a': 2, 'out_b': 3, 'out': 2, 'w': 4}
+LANE_ROW = {'b': 0, 'in': 24, 'out_a': 48, 'out_b': 56}
+TAB_ROW = {'b': ROW_B, 'in': ROW_IN, 'out_a': ROW_OUT, 'out_b': ROW_OUT + 8}
 AHEAD, EARLY_OWN, LAG_MERGE, LAG_FINISH = 2, 3, 2, 3
-LAG_STATS = {'b': (1, 3, 5), 'in': (1, 4, 5), 'out': (1, 2, 3)}
 
 
 def kernel(n_data, n_model, gin_h, gout_h, gq_h, go_h, win_h, wout_h, wq_h, wo_h,
@@ -51,9 +52,9 @@
            w_in, w_out, w_q, w_o, row_in_o, col_in_o, row_out_o, col_out_o, row_q_o, col_q_o, row_o_o, col_o_o,
            row_in, col_in, row_out, col_out, row_q, col_q, row_o, col_o, lane_b, turn,
            gin, gout, gb, part, peer, opp_in, left_in, right_in, grad, w_all, ht,
-           lane_sum, rlane, acc_t, comp_b, tab, rsub, wtab, vtab, mod_in, mod_b, mod_out, mod_w,
-           scal, dat_in, dat_b, dat_out, got_in, got_b, got_out, got_w, got_s,
-           load_sem, w_sem, small_sem, snd, rcv, dsnd, drcv, msnd, mrcv, ssnd, srcv):
+           sum_b, sum_in, sum_a, sum_o, near_b, near_in, both_b, both_in, rlane, acc_t, comp_b, tab, rtab, rsub, wtab, vtab,
+           mod_b, mod_in, mod_a, mod_o, mod_w, scal, dat_b, dat_in, dat_a, dat_o, got_b, got_in, got_a, got_o, got_w, got_s,
+           load_sem, w_sem, small_sem, snd, rcv, psnd, prcv, dsnd, drcv, msnd, mrcv, ssnd, srcv):
     me = lax.axis_index('data')
     mod = lax.axis_index('model')
     n_chips = n_data // 2
@@ -61,14 +62,12 @@
     xr, xl, xo = lax.rem(x + 1, n_chips), lax.rem(x + 3, n_chips), lax.rem(x + 2, n_chips)
     partner, right, left = 2 * x + 1 - c, 2 * xr + c, 2 * xl + c
     full = {'in': n_model * LANES, 'out': n_model * LANES, 'b': n_model * WIDE}
-    count = {'in': N_IN, 'b': N_B, 'out': N_OUT}
-    mats = {'in': N_IN, 'b': 4 * N_B, 'out': N_OUT}
-    first = {'in': FIRST_IN, 'b': FIRST_B, 'out': FIRST_OUT}
-    row0 = {'in': ROW_IN, 'b': ROW_B, 'out': ROW_OUT}
-    mod_blk = {'in': mod_in, 'b': mod_b, 'out': mod_out}
-    dat_got = {'in': dat_in, 'b': dat_b, 'out': dat_out}
-    mod_got = {'in': got_in, 'b': got_b, 'out': got_out}
-    lane_rows = {'in': (0, 24), 'b': (24, 24), 'out': (48, 16)}
+    lane_sum = {'b': sum_b, 'in': sum_in, 'out_a': sum_a, 'out_b': sum_o}
+    near = {'b': near_b, 'in': near_in}
+    both = {'b': both_b, 'in': both_in}
+    dat_got = {'b': dat_b, 'in': dat_in, 'out_a': dat_a, 'out_b': dat_o}
+    mod_blk = {'b': mod_b, 'in': mod_in, 'out_a': mod_a, 'out_b': mod_o}
+    mod_got = {'b': got_b, 'in': got_in, 'out_a': got_a, 'out_b': got_o}
 
     loads = [pltpu.make_async_copy(gq_h.at[pl.ds(0, 8)], gb.at[pl.ds(0, 8)], load_sem.at[0]),
              pltpu.make_async_copy(gq_h.at[pl.ds(8, 46)], gb.at[pl.ds(8, 46)], load_sem.at[1]),
@@ -88,8 +87,8 @@
     barrier = pltpu.get_barrier_semaphore()
 
     def others(axis):
-        side = 2 if axis == 'data' else 4
-        n, rank = (n_data, me) if axis == 'data' else (n_model, mod)
+        side = 4 if axis == 'model' else 2
+        n, rank = (n_model, mod) if axis == 'model' else (n_data, me)
         high, low, rows = lax.div(rank, side), lax.rem(rank, side), n // side
 
         def hops(d):
@@ -97,7 +96,8 @@
             return min(up, rows - up) * (side - 1) + min(over, side - over)
 
         for d in sorted(range(1, n), key=lambda d: -hops(d)):
-            yield lax.rem(high + d // side, rows) * side + lax.rem(low + d % side, side)
+            if axis != 'chip' or d % side == 0:
+                yield lax.rem(high + d // side, rows) * side + lax.rem(low + d % side, side)
 
     for axis in ('model', 'data'):
         for who in others(axis):
@@ -123,7 +123,8 @@
         return remote(src, dst, snd.at[SEND[kind]], rcv.at[RECV[kind], ch], 'data', who)
 
     def convert(ch):
-        family, b0, n = CHUNKS[ch]
+        group, b0, n = CHUNKS[ch]
+        family = GROUPS[group][0]
         if ch == 0:
             loads[0].wait()
         elif ch == 1:
@@ -196,17 +197,16 @@
     lane_iota = lax.broadcasted_iota(jnp.int32, (ROWS, LANES), 1)
 
     def finish(ch):
-        family, b0, n = CHUNKS[ch]
+        group, b0, n = CHUNKS[ch]
+        family, g0, _ = GROUPS[group]
         every = pl.ds(b0, n)
         remote(left_in.at[every], left_in.at[every], snd.at[2], rcv.at[LEFT, ch], 'data', right).wait_recv()
         remote(right_in.at[every], right_in.at[every], snd.at[3], rcv.at[RIGHT, ch], 'data', left).wait_recv()
-        base = lane_rows[family][0] - first[family]
-
         def block(b):
             g = (part[c, x, b] + left_in[b] + right_in[b]) * (1.0 / n_data)
             grad[b] = g
             sq = g * g + EPS_SQ
-            lane_sum[pl.ds(base + b, 1), :] = jnp.sum(sq, axis=0, keepdims=True)
+            lane_sum[group][pl.ds(b - g0, 1), :] = jnp.sum(sq, axis=0, keepdims=True)
             return g, sq
 
         if family == 'b':
@@ -224,19 +224,20 @@
             def body(i, acc):
                 b = b0 + i
                 _, sq = block(b)
-                return jnp.where(lane_iota == b - first[family], jnp.sum(sq, axis=1, keepdims=True), acc)
+                return jnp.where(lane_iota == b - (FIRST_IN if family == 'in' else FIRST_OUT), jnp.sum(sq, axis=1, keepdims=True), acc)
             acc_t[which] = lax.fori_loop(0, n, body, acc_t[which], unroll=2)
 
     def gather(src, dst, sems, slot, axis, op):
         send, recv = sems[0].at[slot], sems[1].at[slot]
-        rank, n = (me, n_data) if axis == 'data' else (mod, n_model)
+        rank, n = {'data': (me, n_data), 'model': (mod, n_model), 'chip': (x, n_chips)}[axis]
+        mesh_axis = 'model' if axis == 'model' else 'data'
         if op == 'start':
             dst[rank] = src[...]
             for who in others(axis):
-                remote(src, dst.at[rank], send, recv, axis, who).start()
+                remote(src, dst.at[rank], send, recv, mesh_axis, who).start()
             return
         rest = dst.at[pl.ds(0, n - 1)]
-        done = remote(rest, rest, send, recv, axis, rank)
+        done = remote(rest, rest, send, recv, mesh_axis, partner if mesh_axis == 'data' else mod)
         if op == 'recv':
             done.wait_recv()
         else:
@@ -250,15 +251,30 @@
 
     d_sems, m_sems, s_sems = (dsnd, drcv), (msnd, mrcv), (ssnd, srcv)
 
-    def lane_ex(family, op):
-        r0, n = lane_rows[family]
-        gather(lane_sum.at[pl.ds(r0, n)], dat_got[family], d_sems, EX_SLOT[family], 'data', op)
-
-    def model_ex(family, op):
-        gather(mod_blk[family], mod_got[family], m_sems, EX_SLOT[family], 'model', op)
+    def pair_ex(group):
+        i = SLOT[group]
+        return remote(lane_sum[group], near[group], psnd.at[i], prcv.at[i], 'data', partner)
+
+    def lane_ex(group, op):
+        pairs = group in near
+        gather((both if pairs else lane_sum)[group], dat_got[group], d_sems, SLOT[group], 'chip' if pairs else 'data', op)
+
+    def lane_start(group):
+        if group in near:
+            pair_ex(group).start()
+        else:
+            lane_ex(group, 'start')
+
+    def lane_pair(group):
+        pair_ex(group).wait_recv()
+        both[group][...] = lane_sum[group][...] + near[group][...]
+        lane_ex(group, 'start')
+
+    def model_ex(group, op):
+        gather(mod_blk[group], mod_got[group], m_sems, SLOT[group], 'model', op)
 
     def scal_ex(family, op):
-        gather(scal.at[EX_SLOT[family]], got_s.at[EX_SLOT[family]], s_sems, EX_SLOT[family], 'data', op)
+        gather(scal.at[SLOT[family]], got_s.at[SLOT[family]], s_sems, SLOT[family], 'data', op)
 
     def weights_start():
         for cp in w_loads + small:
@@ -289,23 +305,27 @@
         vtab[ROW_B + 54:ROW_B + 72, 0:WIDE] = row_o[...]
         mod_w[0:1, :] = jnp.sum(wtab[...].T, axis=0, keepdims=True)
         mod_w[1:2, :] = jnp.sum(vtab[...].T, axis=0, keepdims=True) / n_data
-        gather(mod_w, got_w, m_sems, EX_SLOT['w'], 'model', 'start')
+        gather(mod_w, got_w, m_sems, SLOT['w'], 'model', 'start')
 
     def weights_next():
-        gather(mod_w, got_w, m_sems, EX_SLOT['w'], 'model', 'recv')
-        scal[EX_SLOT['w']] = total(got_w, n_model)
+        gather(mod_w, got_w, m_sems, SLOT['w'], 'model', 'recv')
+        scal[SLOT['w']] = total(got_w, n_model)
         scal_ex('w', 'start')
 
     def weights_done():
         scal_ex('w', 'recv')
-        w_all[...] = total(got_s.at[EX_SLOT['w']], n_data)
-
-    def after_lanes(family):
-        r0, _ = lane_rows[family]
-        n = count[family]
-        lane_ex(family, 'recv')
-        mom, out = {'in': (col_in, col_in_o), 'out': (row_out, row_out_o), 'b': (lane_b, None)}[family]
-        new = BETA_TWO * mom[...] + GAIN * (total(dat_got[family], n_data)[:n] / 512.0)
+        w_all[...] = total(got_s.at[SLOT['w']], n_data)
+
+    def after_lanes(group):
+        family, g0, n = GROUPS[group]
+        r0 = LANE_ROW[group]
+        lane_ex(group, 'recv')
+        lo = g0 - (FIRST_OUT if family == 'out' else g0)
+        if family == 'b':
+            mom = lane_b[...]
+        else:
+            mom = (col_in if family == 'in' else row_out)[lo:lo + n, :]
+        new = BETA_TWO * mom + GAIN * (total(dat_got[group], dat_got[group].shape[0]) / 512.0)
         rlane[r0:r0 + n, :] = lax.rsqrt(new)
         if family == 'b':
             def body(s, carry):
@@ -314,19 +334,17 @@
                 ht[pl.ds(4 * s, 4)] = t
                 comp_b[pl.ds(s, 1), :, ROWS:LANES] = jnp.sum(t * t, axis=1)[None]
                 return carry
-            lax.fori_loop(0, N_B, body, 0, unroll=3)
+            lax.fori_loop(0, n, body, 0, unroll=3)
             mod_b[...] = comp_b[...].reshape(4 * N_B, LANES)
         else:
-            which = 0 if family == 'in' else 1
-
             def body(b, acc):
-                h = grad[first[family] + b] * rlane[pl.ds(r0 + b, 1), :]
-                grad[first[family] + b] = h
-                return jnp.where(lane_iota == b, jnp.sum(h * h, axis=1, keepdims=True), acc)
+                h = grad[g0 + b] * rlane[pl.ds(r0 + b, 1), :]
+                grad[g0 + b] = h
+                return jnp.where(lane_iota == lo + b, jnp.sum(h * h, axis=1, keepdims=True), acc)
             acc_z = lax.fori_loop(0, n, body, jnp.zeros((ROWS, LANES), F32), unroll=4)
-            both = jnp.concatenate([acc_t[which], acc_z], axis=0).T
-            mod_blk[family][...] = both[:mod_blk[family].shape[0]]
-        model_ex(family, 'start')
+            turned = jnp.concatenate([acc_t[0 if family == 'in' else 1], acc_z], axis=0).T
+            mod_blk[group][...] = turned[lo:lo + n]
+        model_ex(group, 'start')
         if family == 'b':
             turn[...] = jnp.zeros_like(turn)
             for q in range(4):
@@ -335,45 +353,48 @@
             turn[...] = turn[...].T
             col_q_o[...] = turn[0:WIDE, 0:N_QKV]
         else:
-            out[...] = new
-
-    def after_model(family):
-        n = mats[family]
-        model_ex(family, 'recv')
-        both = total(mod_got[family], n_model)[:n]
-        sums, z = both[:, 0:ROWS], both[:, ROWS:LANES]
+            (col_in_o if family == 'in' else row_out_o)[lo:lo + n, :] = new
+
+    def after_model(group):
+        family, g0, n = GROUPS[group]
+        lo = g0 - (FIRST_OUT if family == 'out' else g0)
+        model_ex(group, 'recv')
+        sums_z = total(mod_got[group], n_model)
+        sums, z = sums_z[:, 0:ROWS], sums_z[:, ROWS:LANES]
         if family == 'b':
             mom = jnp.concatenate([row_q[...], col_o[...]], axis=0)
         else:
-            mom = (row_in if family == 'in' else col_out)[...]
+            mom = (row_in if family == 'in' else col_out)[lo:lo + n, :]
         new = BETA_TWO * mom + GAIN * (sums / full[family])
-        ratio = z / new
         mean_part = GAIN * (sums / 512.0)
         if family == 'in':
             term = new
         elif family == 'out':
             term = mean_part
         else:
-            term = jnp.where(lax.broadcasted_iota(jnp.int32, (n, ROWS), 0) < 54, new, mean_part)
-        r0 = row0[family]
-        tab[r0:r0 + n, 0:ROWS] = ratio
-        tab[r0:r0 + n, ROWS:LANES] = term
+            term = jnp.where(lax.broadcasted_iota(jnp.int32, new.shape, 0) < N_QKV, new, mean_part)
+        r0 = TAB_ROW[group]
+        r1 = r0 + new.shape[0]
+        tab[r0:r1, 0:ROWS] = z / new
+        tab[r0:r1, ROWS:LANES] = term
+        rtab[r0:r1, 0:ROWS] = lax.rsqrt(new)
+        if family == 'b':
+            row_q_o[...] = new[:N_QKV]
+            col_o_o[...] = new[N_QKV:]
+        else:
+            (row_in_o if family == 'in' else col_out_o)[lo:lo + n, :] = new
+
+    def scalars_start(family):
+        e = SLOT[family]
         turned = tab[...].T
-        e = EX_SLOT[family]
         scal[e, 0:1, :] = jnp.sum(turned[:ROWS], axis=0, keepdims=True)
         scal[e, 1:2, :] = jnp.sum(turned[ROWS:], axis=0, keepdims=True)
         scal_ex(family, 'start')
-        if family == 'b':
-            row_q_o[...] = new[:N_QKV]
-            col_o_o[...] = new[N_QKV:]
-            rsub[e, r0:r0 + n, 0:ROWS] = lax.rsqrt(new)
-        else:
-            (row_in_o if family == 'in' else col_out_o)[...] = new
-            tab[r0:r0 + n, 0:ROWS] = lax.rsqrt(new)
-            rsub[e] = tab[...].T
+        if family != 'b':
+            rsub[...] = rtab[:, 0:ROWS].T
 
     def after_scalars(family):
-        e = EX_SLOT[family]
+        e = SLOT[family]
         scal_ex(family, 'recv')
         tot = total(got_s.at[e], n_data)
         q, s = tot[0:1], tot[1:2]
@@ -382,45 +403,44 @@
         size = 512.0 * full[family]
         m = (s if family == 'in' else BETA_TWO * v + s) / rows
         scale = jnp.sqrt(m) * (LR_BASE * jnp.maximum(1e-3, jnp.sqrt(w / size))) / jnp.maximum(1.0, jnp.sqrt(m * q / size))
-        r0 = row0[family]
-        if family == 'b':
-            n = mats[family]
-            tab[...] = jnp.broadcast_to(scale, (LANES, LANES)).T
-            rsub[e, r0:r0 + n, 0:ROWS] = rsub[e, r0:r0 + n, 0:ROWS] * tab[r0:r0 + n, 0:ROWS]
-
+        if family == 'b':
+            turn[...] = jnp.broadcast_to(scale, (LANES, LANES)).T
+            rtab[ROW_B:ROW_B + 72, 0:ROWS] = rtab[ROW_B:ROW_B + 72, 0:ROWS] * turn[ROW_B:ROW_B + 72, 0:ROWS]
             for ref, b0 in ((w_q, 0), (w_o, N_QKV)):
                 def body(b, carry, ref=ref, b0=b0):
-                    ref[b] = ref[b] - ht[b0 + b] * rsub[e, pl.ds(r0 + b0 + b, 1), 0:ROWS]
+                    ref[b] = ref[b] - ht[b0 + b] * rtab[pl.ds(ROW_B + b0 + b, 1), 0:ROWS]
                     return carry
                 lax.fori_loop(0, ref.shape[0], body, 0, unroll=6)
         else:
-            ref = w_in if family == 'in' else w_out
-            fac = rsub[e, 0:ROWS, :] * scale
+            ref, r0, g0 = (w_in, ROW_IN, FIRST_IN) if family == 'in' else (w_out, ROW_OUT, FIRST_OUT)
+            fac = rsub[...] * scale
 
             def body(b, carry):
                 f = jnp.sum(jnp.where(lane_iota == r0 + b, fac, 0.0), axis=1, keepdims=True)
-                ref[b] = ref[b] - grad[first[family] + b] * f
+                ref[b] = ref[b] - grad[g0 + b] * f
                 return carry
-            lax.fori_loop(0, count[family], body, 0, unroll=4)
+            lax.fori_loop(0, ref.shape[0], body, 0, unroll=4)
 
     def sent_early():
         for i, ref in enumerate((peer, opp_in, left_in, right_in)):
             remote(ref, ref, snd.at[i], rcv.at[0, 0], 'data', partner).wait_send()
-        gather(mod_w, got_w, m_sems, EX_SLOT['w'], 'model', 'send')
-        scal_ex('w', 'send')
-        for family in ('b', 'in'):
-            lane_ex(family, 'send')
-            model_ex(family, 'send')
+        gather(mod_w, got_w, m_sems, SLOT['w'], 'model', 'send')
+        for group in near:
+            pair_ex(group).wait_send()
+        for group in GROUPS:
+            lane_ex(group, 'send')
+            if group != 'out_b':
+                model_ex(group, 'send')
+        for family in ('w', 'b', 'in'):
             scal_ex(family, 'send')
 
     def sent_late():
-        lane_ex('out', 'send')
-        model_ex('out', 'send')
+        model_ex('out_b', 'send')
         scal_ex('out', 'send')
 
     acc_t[...] = jnp.zeros_like(acc_t)
     tab[...] = jnp.zeros_like(tab)
-    lane_sum[...] = jnp.zeros_like(lane_sum)
+    rtab[...] = jnp.zeros_like(rtab)
 
     convert(0)
     for cp in small + w_loads:
@@ -428,7 +448,25 @@
     pl.semaphore_wait(barrier, n_data - 1 + n_model - 1)
     transfer(D2D, 0).start()
     last = N_CH - 1 + LAG_FINISH
-    for k in range(1 - AHEAD, last + 1 + LAG_STATS['out'][2]):
+    steps = {}
+
+    def at(k, do, *args):
+        steps.setdefault(k, []).append((do, args))
+
+    at(4, weights_start)
+    at(6, weights_next)
+    at(8, weights_done)
+    k_b, k_in, k_a = (LAST_CHUNK[g] + LAG_FINISH for g in ('b', 'in', 'out_a'))
+    at(k_b + 1, lane_pair, 'b')
+    at(k_b + 3, after_lanes, 'b')
+    at(k_b + 5, after_model, 'b')
+    at(k_b + 5, scalars_start, 'b')
+    at(k_b + 7, after_scalars, 'b')
+    at(k_in + 1, lane_pair, 'in')
+    at(k_in + 3, after_lanes, 'in')
+    tail = ((after_lanes, 'out_a'), (after_lanes, 'out_b'), (after_model, 'in'), (scalars_start, 'in'), (after_model, 'out_a'),
+            (sent_early,), (after_model, 'out_b'), (scalars_start, 'out'), (after_scalars, 'in'), (after_scalars, 'out'), (sent_late,))
+    for k in range(1 - AHEAD, last + 1):
         if 0 <= k < N_CH:
             opposite(k)
         if k + AHEAD < N_CH:
@@ -437,28 +475,15 @@
         for ch in range(N_CH):
             if k == ch + (LAG_MERGE if ch < N_CH - 1 else 1):
                 merge(ch)
-        if k == 4:
-            weights_start()
-        if k == 6:
-            weights_next()
-        if k == 8:
-            weights_done()
-        if k == last + 2:
-            sent_early()
-        for family in GROUPS:
-            after = k - (LAST_CHUNK[family] + LAG_FINISH)
-            if after == LAG_STATS[family][0]:
-                after_lanes(family)
-            if after == LAG_STATS[family][1]:
-                after_model(family)
-            if after == LAG_STATS[family][2]:
-                after_scalars(family)
+        for do, args in steps.get(k, ()):
+            do(*args)
         if 0 <= k - LAG_FINISH < N_CH:
             finish(k - LAG_FINISH)
-        for family in GROUPS:
-            if k == LAST_CHUNK[family] + LAG_FINISH:
-                lane_ex(family, 'start')
-    sent_late()
+        for group in GROUPS:
+            if k == LAST_CHUNK[group] + LAG_FINISH:
+                lane_start(group)
+    for do, *args in tail:
+        do(*args)
 
 
 def deliver(*refs):
@@ -489,15 +514,17 @@
         vmem(2, n_chips, N_SUP, ROWS, LANES), vmem(n_chips, N_SUP, ROWS, LANES),
         vmem(N_SUP, ROWS, LANES), vmem(N_SUP, ROWS, LANES), vmem(N_SUP, ROWS, LANES), vmem(N_SUP, ROWS, LANES),
         vmem(2, LANES), vmem(72, WIDE, ROWS),
-        vmem(ROWS, LANES), vmem(ROWS, LANES), vmem(2, ROWS, LANES), vmem(N_B, 4, LANES),
-        vmem(LANES, LANES), vmem(3, LANES, LANES), vmem(LANES, LANES), vmem(LANES, LANES),
-        vmem(24, LANES), vmem(72, LANES), vmem(16, LANES), vmem(2, LANES),
-        vmem(4, 2, LANES), vmem(n_data, 24, LANES), vmem(n_data, 24, LANES), vmem(n_data, 16, LANES),
-        vmem(n_model, 24, LANES), vmem(n_model, 72, LANES), vmem(n_model, 16, LANES), vmem(n_model, 2, LANES),
-        vmem(4, n_data, 2, LANES),
+        vmem(18, LANES), vmem(24, LANES), vmem(8, LANES), vmem(4, LANES),
+        vmem(18, LANES), vmem(24, LANES), vmem(18, LANES), vmem(24, LANES),
+        vmem(ROWS, LANES), vmem(2, ROWS, LANES), vmem(N_B, 4, LANES),
+        vmem(LANES, LANES), vmem(LANES, LANES), vmem(ROWS, LANES), vmem(LANES, LANES), vmem(LANES, LANES),
+        vmem(72, LANES), vmem(24, LANES), vmem(8, LANES), vmem(4, LANES), vmem(2, LANES), vmem(5, 2, LANES),
+        vmem(n_chips, 18, LANES), vmem(n_chips, 24, LANES), vmem(n_data, 8, LANES), vmem(n_data, 4, LANES),
+        vmem(n_model, 72, LANES), vmem(n_model, 24, LANES), vmem(n_model, 8, LANES), vmem(n_model, 4, LANES),
+        vmem(n_model, 2, LANES), vmem(5, n_data, 2, LANES),
         pltpu.SemaphoreType.DMA((5,)), pltpu.SemaphoreType.DMA((4,)), pltpu.SemaphoreType.DMA((8,)),
         pltpu.SemaphoreType.DMA((4,)), pltpu.SemaphoreType.DMA((5, N_CH)),
-        *(pltpu.SemaphoreType.DMA((n,)) for n in (3, 3, 4, 4, 4, 4)),
+        *(pltpu.SemaphoreType.DMA((n,)) for n in (2, 2, 4, 4, 5, 5, 5, 5)),
     ]
     hbm, in_vmem = pl.BlockSpec(memory_space=pltpu.HBM), pl.BlockSpec(memory_space=pltpu.VMEM)
 

time: 86.7 us -> 85.3 us (0.984)
  Pallas kernels: 85.9 us -> 84.5 us
    pallas_call x1, Pallas kernels: 84.4 us -> 83 us  [step_all(): pl.pallas_call(functools.partial(kernel, n_data, n_model), name='adafacto...]
where the time goes in v4:
time: 85.3 us; the launch traced here: 85.2 us
  Pallas kernels  84.5 us (99%)
    pallas_call x1, Pallas kernels, step_all(): pl.pallas_call(functools.partial(kernel, n_data, n_model), name='adafacto...  83 us

profile of v4, /device:TPU:1, one launch (start us, length us, event | category | flops | bytes accessed | tf_op | source)
XLA Modules:
  0.0 85.2 jit_solution(11826006418585374498)
XLA Ops:
  0.7 83.0 %adafactor_step.1 = (f32[24,64,128]{2,1,0:T(8,128)S(1)}, f32[12,64,128]{2,1,0:T(8,128)S(1)}, f32[54,32,64]{2,1,0:T(8,128)S(1)}, f32[18,32,64]{2,1,0:T(8,128)S(1)...) custom-call(bf16[24,512,128]{2,1,0:T(8,128)(2,1)} %bitcast.12, ...), custom_call_target="tpu_custom_call" | custom-call | tf_op jit(solution)/shard_map/adafactor_step/pallas_call | solution.py:533
  83.7 1.5 %deliver.1 = (f32[24,64,128]{2,1,0:T(8,128)}, f32[12,64,128]{2,1,0:T(8,128)}, f32[54,32,64]{2,1,0:T(8,128)}, f32[18,32,64]{2,1,0:T(8,128)}, f32[24,64]{1,0:T(8,1...) custom-call(f32[24,64,128]{2,1,0:T(8,128)S(1)} %get-tuple-element.36, ...), custom_call_target="tpu_custom_call" | custom-call | tf_op jit(solution)/shard_map/deliver/pallas_call | solution.py:545

commit v5 on v4

--- a/solution.py
+++ b/solution.py
@@ -20,9 +20,11 @@
 N_SUP = N_IN + N_B + N_OUT
 FIRST_B, FIRST_IN, FIRST_OUT = 0, N_B, N_B + N_IN
 N_QKV, N_O = 54, 18
+N_OUT_B = 2
+N_OUT_A = N_OUT - N_OUT_B
 ROW_IN, ROW_OUT, ROW_B = 0, 24, 40
-GROUPS = {'b': ('b', FIRST_B, N_B), 'in': ('in', FIRST_IN, N_IN), 'out_a': ('out', FIRST_OUT, 8), 'out_b': ('out', FIRST_OUT + 8, 4)}
-SIZES = (('b', (2, 4, 6, 6)), ('in', (6, 6, 6, 6)), ('out_a', (4, 4)), ('out_b', (2, 2)))
+GROUPS = {'b': ('b', FIRST_B, N_B), 'in': ('in', FIRST_IN, N_IN), 'out_a': ('out', FIRST_OUT, N_OUT_A), 'out_b': ('out', FIRST_OUT + N_OUT_A, N_OUT_B)}
+SIZES = (('b', (2, 4, 6, 6)), ('in', (6, 6, 6, 6)), ('out_a', (4, 4, 2)), ('out_b', (2,)))
 
 
 def cut():
@@ -39,11 +41,11 @@
 LAST_CHUNK = {g: max(i for i, c in enumerate(CHUNKS) if c[0] == g) for g in GROUPS}
 D2D, OPP_A, OPP_B, OWN_R, OWN_L, MRG_R, MRG_L = range(7)
 SEND = (0, 1, 1, 2, 3, 2, 3)
-LEFT, RIGHT = 3, 4
-RECV = (D2D, OPP_A, OPP_B, LEFT, RIGHT, LEFT, RIGHT)
-SLOT = {'b': 0, 'in': 1, 'out_a': 2, 'out_b': 3, 'out': 2, 'w': 4}
-LANE_ROW = {'b': 0, 'in': 24, 'out_a': 48, 'out_b': 56}
-TAB_ROW = {'b': ROW_B, 'in': ROW_IN, 'out_a': ROW_OUT, 'out_b': ROW_OUT + 8}
+OPP, LAST = 1, 2
+RECV = (D2D, OPP, OPP, LAST, LAST, LAST, LAST)
+SLOT = {'b': 0, 'in': 1, 'out_a': 2, 'out_b': 3, 'w': 4}
+LANE_ROW = {'b': 0, 'in': 24, 'out_a': 48, 'out_b': 48 + N_OUT_A}
+TAB_ROW = {'b': ROW_B, 'in': ROW_IN, 'out_a': ROW_OUT, 'out_b': ROW_OUT + N_OUT_A}
 AHEAD, EARLY_OWN, LAG_MERGE, LAG_FINISH = 2, 3, 2, 3
 
 
@@ -52,9 +54,10 @@
            w_in, w_out, w_q, w_o, row_in_o, col_in_o, row_out_o, col_out_o, row_q_o, col_q_o, row_o_o, col_o_o,
            row_in, col_in, row_out, col_out, row_q, col_q, row_o, col_o, lane_b, turn,
            gin, gout, gb, part, peer, opp_in, left_in, right_in, grad, w_all, ht,
-           sum_b, sum_in, sum_a, sum_o, near_b, near_in, both_b, both_in, rlane, acc_t, comp_b, tab, rtab, rsub, wtab, vtab,
+           sum_b, sum_in, sum_a, sum_o, near_b, near_in, both_b, both_in, full_b, full_in, rlane, acc_t, comp_b, tab, rtab, rsub, wtab, vtab,
            mod_b, mod_in, mod_a, mod_o, mod_w, scal, dat_b, dat_in, dat_a, dat_o, got_b, got_in, got_a, got_o, got_w, got_s,
-           load_sem, w_sem, small_sem, snd, rcv, psnd, prcv, dsnd, drcv, msnd, mrcv, ssnd, srcv):
+           raw_a, raw_o, graw_a, graw_o, wcol, krow,
+           load_sem, w_sem, small_sem, first_sem, snd, rcv, psnd, prcv, bsnd, brcv, dsnd, drcv, msnd, mrcv, ssnd, srcv):
     me = lax.axis_index('data')
     mod = lax.axis_index('model')
     n_chips = n_data // 2
@@ -65,8 +68,11 @@
     lane_sum = {'b': sum_b, 'in': sum_in, 'out_a': sum_a, 'out_b': sum_o}
     near = {'b': near_b, 'in': near_in}
     both = {'b': both_b, 'in': both_in}
+    whole = {'b': full_b, 'in': full_in}
     dat_got = {'b': dat_b, 'in': dat_in, 'out_a': dat_a, 'out_b': dat_o}
     mod_blk = {'b': mod_b, 'in': mod_in, 'out_a': mod_a, 'out_b': mod_o}
+    raw = {'out_a': raw_a, 'out_b': raw_o}
+    raw_got = {'out_a': graw_a, 'out_b': graw_o}
     mod_got = {'b': got_b, 'in': got_in, 'out_a': got_a, 'out_b': got_o}
 
     loads = [pltpu.make_async_copy(gq_h.at[pl.ds(0, 8)], gb.at[pl.ds(0, 8)], load_sem.at[0]),
@@ -151,6 +157,15 @@
 
         lax.fori_loop(0, n, body, 0)
 
+    def first_pair(dest, sem):
+        every = pl.ds(0, CHUNKS[0][2])
+        return remote(part.at[1 - c, dest, every], peer.at[dest, every], snd.at[0], sem, 'data', partner)
+
+    def first_pairs():
+        first_pair(xo, first_sem.at[0]).start()
+        for dest in (xr, xl, x):
+            first_pair(dest, rcv.at[D2D, 0]).start()
+
     def add_peer(ch, dest):
         _, b0, n = CHUNKS[ch]
 
@@ -161,10 +176,16 @@
         lax.fori_loop(0, n, body, 0, unroll=2)
 
     def opposite(ch):
-        transfer(D2D, ch).wait_recv()
+        if ch == 0:
+            first_pair(xo, first_sem.at[0]).wait_recv()
+        else:
+            transfer(D2D, ch).wait_recv()
         add_peer(ch, xo)
         transfer(OPP_A, ch).start()
         transfer(OPP_B, ch).start()
+        if ch == 0:
+            rest = peer.at[pl.ds(0, n_chips - 1), pl.ds(0, CHUNKS[0][2])]
+            remote(rest, rest, snd.at[0], rcv.at[D2D, 0], 'data', partner).wait_recv()
         add_peer(ch, xr)
         add_peer(ch, xl)
         if ch < EARLY_OWN:
@@ -185,10 +206,10 @@
                 return carry
             lax.fori_loop(lo, hi, body, 0)
 
-        transfer(OPP_A, ch).wait_recv()
+        every = opp_in.at[pl.ds(b0, n)]
+        remote(every, every, snd.at[1], rcv.at[OPP, ch], 'data', left).wait_recv()
         add(xr, b0, b0 + n_a)
         transfer(MRG_R, ch).start()
-        transfer(OPP_B, ch).wait_recv()
         add(xl, b0 + n_a, b0 + n)
         transfer(MRG_L, ch).start()
         if ch >= EARLY_OWN:
@@ -200,13 +221,19 @@
         group, b0, n = CHUNKS[ch]
         family, g0, _ = GROUPS[group]
         every = pl.ds(b0, n)
-        remote(left_in.at[every], left_in.at[every], snd.at[2], rcv.at[LEFT, ch], 'data', right).wait_recv()
-        remote(right_in.at[every], right_in.at[every], snd.at[3], rcv.at[RIGHT, ch], 'data', left).wait_recv()
+        two = peer.at[pl.ds(0, 2), every]
+        remote(two, two, snd.at[2], rcv.at[LAST, ch], 'data', right).wait_recv()
+
         def block(b):
             g = (part[c, x, b] + left_in[b] + right_in[b]) * (1.0 / n_data)
             grad[b] = g
             sq = g * g + EPS_SQ
-            lane_sum[group][pl.ds(b - g0, 1), :] = jnp.sum(sq, axis=0, keepdims=True)
+            sums = jnp.sum(sq, axis=0, keepdims=True)
+            if group in near:
+                half = lane_sum[group].shape[1]
+                lane_sum[group][lax.div(b - g0, half), pl.ds(lax.rem(b - g0, half), 1), :] = sums
+            else:
+                lane_sum[group][pl.ds(b - g0, 1), :] = sums
             return g, sq
 
         if family == 'b':
@@ -257,7 +284,16 @@
 
     def lane_ex(group, op):
         pairs = group in near
-        gather((both if pairs else lane_sum)[group], dat_got[group], d_sems, SLOT[group], 'chip' if pairs else 'data', op)
+        gather(both[group].at[c] if pairs else lane_sum[group], dat_got[group], d_sems, SLOT[group], 'chip' if pairs else 'data', op)
+
+    def back_ex(group):
+        i = SLOT[group]
+        return remote(whole[group].at[c], whole[group].at[c], bsnd.at[i], brcv.at[i], 'data', partner)
+
+    def lane_back(group):
+        lane_ex(group, 'recv')
+        whole[group][c] = total(dat_got[group], n_chips)
+        back_ex(group).start()
 
     def lane_start(group):
         if group in near:
@@ -273,8 +309,10 @@
     def model_ex(group, op):
         gather(mod_blk[group], mod_got[group], m_sems, SLOT[group], 'model', op)
 
-    def scal_ex(family, op):
-        gather(scal.at[SLOT[family]], got_s.at[SLOT[family]], s_sems, SLOT[family], 'data', op)
+    def scal_ex(name, op):
+        i = SLOT[name]
+        src, dst = (raw[name], raw_got[name]) if name in raw else (scal.at[i], got_s.at[i])
+        gather(src, dst, s_sems, i, 'data', op)
 
     def weights_start():
         for cp in w_loads + small:
@@ -315,17 +353,24 @@
     def weights_done():
         scal_ex('w', 'recv')
         w_all[...] = total(got_s.at[SLOT['w']], n_data)
+        turn[0:2, :] = w_all[...]
+        wcol[...] = turn[...].T
 
     def after_lanes(group):
         family, g0, n = GROUPS[group]
         r0 = LANE_ROW[group]
-        lane_ex(group, 'recv')
+        if group in near:
+            back_ex(group).wait_recv()
+            sums = jnp.concatenate([whole[group][0], whole[group][1]], axis=0)
+        else:
+            lane_ex(group, 'recv')
+            sums = total(dat_got[group], n_data)
         lo = g0 - (FIRST_OUT if family == 'out' else g0)
         if family == 'b':
             mom = lane_b[...]
         else:
             mom = (col_in if family == 'in' else row_out)[lo:lo + n, :]
-        new = BETA_TWO * mom + GAIN * (total(dat_got[group], dat_got[group].shape[0]) / 512.0)
+        new = BETA_TWO * mom + GAIN * (sums / 512.0)
         rlane[r0:r0 + n, :] = lax.rsqrt(new)
         if family == 'b':
             def body(s, carry):
@@ -375,8 +420,13 @@
             term = jnp.where(lax.broadcasted_iota(jnp.int32, new.shape, 0) < N_QKV, new, mean_part)
         r0 = TAB_ROW[group]
         r1 = r0 + new.shape[0]
-        tab[r0:r1, 0:ROWS] = z / new
-        tab[r0:r1, ROWS:LANES] = term
+        if family == 'out':
+            raw[group][:, 0:ROWS] = z / new
+            raw[group][:, ROWS:LANES] = term
+            scal_ex(group, 'start')
+        else:
+            tab[r0:r1, 0:ROWS] = z / new
+            tab[r0:r1, ROWS:LANES] = term
         rtab[r0:r1, 0:ROWS] = lax.rsqrt(new)
         if family == 'b':
             row_q_o[...] = new[:N_QKV]
@@ -393,16 +443,17 @@
         if family != 'b':
             rsub[...] = rtab[:, 0:ROWS].T
 
+    def factor(q, s, w, v, family):
+        rows = 512.0 if family == 'in' else float(full[family])
+        size = 512.0 * full[family]
+        m = (s if family == 'in' else BETA_TWO * v + s) / rows
+        return jnp.sqrt(m) * (LR_BASE * jnp.maximum(1e-3, jnp.sqrt(w / size))) / jnp.maximum(1.0, jnp.sqrt(m * q / size))
+
     def after_scalars(family):
         e = SLOT[family]
         scal_ex(family, 'recv')
         tot = total(got_s.at[e], n_data)
-        q, s = tot[0:1], tot[1:2]
-        w, v = w_all[0:1, :], w_all[1:2, :]
-        rows = 512.0 if family == 'in' else float(full[family])
-        size = 512.0 * full[family]
-        m = (s if family == 'in' else BETA_TWO * v + s) / rows
-        scale = jnp.sqrt(m) * (LR_BASE * jnp.maximum(1e-3, jnp.sqrt(w / size))) / jnp.maximum(1.0, jnp.sqrt(m * q / size))
+        scale = factor(tot[0:1], tot[1:2], w_all[0:1, :], w_all[1:2, :], family)
         if family == 'b':
             turn[...] = jnp.broadcast_to(scale, (LANES, LANES)).T
             rtab[ROW_B:ROW_B + 72, 0:ROWS] = rtab[ROW_B:ROW_B + 72, 0:ROWS] * turn[ROW_B:ROW_B + 72, 0:ROWS]
@@ -412,14 +463,34 @@
                     return carry
                 lax.fori_loop(0, ref.shape[0], body, 0, unroll=6)
         else:
-            ref, r0, g0 = (w_in, ROW_IN, FIRST_IN) if family == 'in' else (w_out, ROW_OUT, FIRST_OUT)
             fac = rsub[...] * scale
 
             def body(b, carry):
-                f = jnp.sum(jnp.where(lane_iota == r0 + b, fac, 0.0), axis=1, keepdims=True)
-                ref[b] = ref[b] - grad[g0 + b] * f
+                f = jnp.sum(jnp.where(lane_iota == ROW_IN + b, fac, 0.0), axis=1, keepdims=True)
+                w_in[b] = w_in[b] - grad[FIRST_IN + b] * f
                 return carry
-            lax.fori_loop(0, ref.shape[0], body, 0, unroll=4)
+            lax.fori_loop(0, N_IN, body, 0, unroll=4)
+
+    def prepare_out():
+        fac = rtab[:, 0:ROWS].T
+
+        def body(b, carry):
+            f = jnp.sum(jnp.where(lane_iota == ROW_OUT + b, fac, 0.0), axis=1, keepdims=True)
+            grad[FIRST_OUT + b] = grad[FIRST_OUT + b] * f
+            return carry
+        lax.fori_loop(0, N_OUT, body, 0, unroll=4)
+
+    def apply_out(group):
+        _, g0, n = GROUPS[group]
+        lo, r0 = g0 - FIRST_OUT, TAB_ROW[group]
+        scal_ex(group, 'recv')
+        tot = total(raw_got[group], n_data)
+        q = jnp.sum(tot[:, 0:ROWS], axis=1, keepdims=True)
+        s = jnp.sum(tot[:, ROWS:LANES], axis=1, keepdims=True)
+        scale = factor(q, s, wcol[r0:r0 + n, 0:1], wcol[r0:r0 + n, 1:2], 'out')
+        krow[lo:lo + n, :] = jnp.broadcast_to(scale, (n, LANES))
+        for b in range(lo, lo + n):
+            w_out[b] = w_out[b] - grad[FIRST_OUT + b] * krow[b:b + 1, :]
 
     def sent_early():
         for i, ref in enumerate((peer, opp_in, left_in, right_in)):
@@ -427,16 +498,21 @@
         gather(mod_w, got_w, m_sems, SLOT['w'], 'model', 'send')
         for group in near:
             pair_ex(group).wait_send()
+            back_ex(group).wait_send()
         for group in GROUPS:
             lane_ex(group, 'send')
-            if group != 'out_b':
-                model_ex(group, 'send')
-        for family in ('w', 'b', 'in'):
-            scal_ex(family, 'send')
+        model_ex('b', 'send')
+        scal_ex('w', 'send')
+        scal_ex('b', 'send')
+
+    def sent_mid():
+        for group in ('in', 'out_a', 'out_b'):
+            model_ex(group, 'send')
+        scal_ex('in', 'send')
+        scal_ex('out_a', 'send')
 
     def sent_late():
-        model_ex('out_b', 'send')
-        scal_ex('out', 'send')
+        scal_ex('out_b', 'send')
 
     acc_t[...] = jnp.zeros_like(acc_t)
     tab[...] = jnp.zeros_like(tab)
@@ -446,7 +522,7 @@
     for cp in small + w_loads:
         cp.start()
     pl.semaphore_wait(barrier, n_data - 1 + n_model - 1)
-    transfer(D2D, 0).start()
+    first_pairs()
     last = N_CH - 1 + LAG_FINISH
     steps = {}
 
@@ -458,14 +534,15 @@
     at(8, weights_done)
     k_b, k_in, k_a = (LAST_CHUNK[g] + LAG_FINISH for g in ('b', 'in', 'out_a'))
     at(k_b + 1, lane_pair, 'b')
-    at(k_b + 3, after_lanes, 'b')
-    at(k_b + 5, after_model, 'b')
-    at(k_b + 5, scalars_start, 'b')
-    at(k_b + 7, after_scalars, 'b')
+    at(k_b + 3, lane_back, 'b')
+    at(k_b + 4, after_lanes, 'b')
+    at(k_b + 6, after_model, 'b')
+    at(k_b + 6, scalars_start, 'b')
     at(k_in + 1, lane_pair, 'in')
-    at(k_in + 3, after_lanes, 'in')
-    tail = ((after_lanes, 'out_a'), (after_lanes, 'out_b'), (after_model, 'in'), (scalars_start, 'in'), (after_model, 'out_a'),
-            (sent_early,), (after_model, 'out_b'), (scalars_start, 'out'), (after_scalars, 'in'), (after_scalars, 'out'), (sent_late,))
+    at(k_in + 3, lane_back, 'in')
+    tail = ((after_lanes, 'in'), (after_lanes, 'out_a'), (after_lanes, 'out_b'), (after_scalars, 'b'), (sent_early,), (after_model, 'in'),
+            (scalars_start, 'in'), (after_model, 'out_a'), (after_model, 'out_b'), (prepare_out,), (sent_mid,), (after_scalars, 'in'),
+            (apply_out, 'out_a'), (apply_out, 'out_b'), (sent_late,))
     for k in range(1 - AHEAD, last + 1):
         if 0 <= k < N_CH:
             opposite(k)
@@ -514,17 +591,18 @@
         vmem(2, n_chips, N_SUP, ROWS, LANES), vmem(n_chips, N_SUP, ROWS, LANES),
         vmem(N_SUP, ROWS, LANES), vmem(N_SUP, ROWS, LANES), vmem(N_SUP, ROWS, LANES), vmem(N_SUP, ROWS, LANES),
         vmem(2, LANES), vmem(72, WIDE, ROWS),
-        vmem(18, LANES), vmem(24, LANES), vmem(8, LANES), vmem(4, LANES),
-        vmem(18, LANES), vmem(24, LANES), vmem(18, LANES), vmem(24, LANES),
+        vmem(2, 9, LANES), vmem(2, 12, LANES), vmem(N_OUT_A, LANES), vmem(N_OUT_B, LANES),
+        *(vmem(2, n, LANES) for n in (9, 12, 9, 12, 9, 12)),
         vmem(ROWS, LANES), vmem(2, ROWS, LANES), vmem(N_B, 4, LANES),
         vmem(LANES, LANES), vmem(LANES, LANES), vmem(ROWS, LANES), vmem(LANES, LANES), vmem(LANES, LANES),
-        vmem(72, LANES), vmem(24, LANES), vmem(8, LANES), vmem(4, LANES), vmem(2, LANES), vmem(5, 2, LANES),
-        vmem(n_chips, 18, LANES), vmem(n_chips, 24, LANES), vmem(n_data, 8, LANES), vmem(n_data, 4, LANES),
-        vmem(n_model, 72, LANES), vmem(n_model, 24, LANES), vmem(n_model, 8, LANES), vmem(n_model, 4, LANES),
+        vmem(72, LANES), vmem(24, LANES), vmem(N_OUT_A, LANES), vmem(N_OUT_B, LANES), vmem(2, LANES), vmem(5, 2, LANES),
+        vmem(n_chips, 9, LANES), vmem(n_chips, 12, LANES), vmem(n_data, N_OUT_A, LANES), vmem(n_data, N_OUT_B, LANES),
+        vmem(n_model, 72, LANES), vmem(n_model, 24, LANES), vmem(n_model, N_OUT_A, LANES), vmem(n_model, N_OUT_B, LANES),
         vmem(n_model, 2, LANES), vmem(5, n_data, 2, LANES),
-        pltpu.SemaphoreType.DMA((5,)), pltpu.SemaphoreType.DMA((4,)), pltpu.SemaphoreType.DMA((8,)),
-        pltpu.SemaphoreType.DMA((4,)), pltpu.SemaphoreType.DMA((5, N_CH)),
-        *(pltpu.SemaphoreType.DMA((n,)) for n in (2, 2, 4, 4, 5, 5, 5, 5)),
+        vmem(N_OUT_A, LANES), vmem(N_OUT_B, LANES), vmem(n_data, N_OUT_A, LANES), vmem(n_data, N_OUT_B, LANES), vmem(LANES, LANES), vmem(12, LANES),
+        pltpu.SemaphoreType.DMA((5,)), pltpu.SemaphoreType.DMA((4,)), pltpu.SemaphoreType.DMA((8,)), pltpu.SemaphoreType.DMA((1,)),
+        pltpu.SemaphoreType.DMA((4,)), pltpu.SemaphoreType.DMA((3, N_CH)),
+        *(pltpu.SemaphoreType.DMA((n,)) for n in (2, 2, 2, 2, 4, 4, 5, 5, 5, 5)),
     ]
     hbm, in_vmem = pl.BlockSpec(memory_space=pltpu.HBM), pl.BlockSpec(memory_space=pltpu.VMEM)
 

time: 85.3 us -> 84 us (0.985)
  Pallas kernels: 84.5 us -> 83.3 us
    pallas_call x1, Pallas kernels: 83 us -> 81.7 us  [step_all(): pl.pallas_call(functools.partial(kernel, n_data, n_model), name='adafacto...]
where the time goes in v5:
time: 84 us; the launch traced here: 83.9 us
  Pallas kernels  83.3 us (99%)
    pallas_call x1, Pallas kernels, step_all(): pl.pallas_call(functools.partial(kernel, n_data, n_model), name='adafacto...  81.7 us

profile of v5, /device:TPU:1, one launch (start us, length us, event | category | flops | bytes accessed | tf_op | source)
XLA Modules:
  0.0 83.9 jit_solution(1807160692429416890)
XLA Ops:
  0.7 81.7 %adafactor_step.1 = (f32[24,64,128]{2,1,0:T(8,128)S(1)}, f32[12,64,128]{2,1,0:T(8,128)S(1)}, f32[54,32,64]{2,1,0:T(8,128)S(1)}, f32[18,32,64]{2,1,0:T(8,128)S(1)...) custom-call(bf16[24,512,128]{2,1,0:T(8,128)(2,1)} %bitcast.12, ...), custom_call_target="tpu_custom_call" | custom-call | tf_op jit(solution)/shard_map/adafactor_step/pallas_call | solution.py:611
  82.4 1.5 %deliver.1 = (f32[24,64,128]{2,1,0:T(8,128)}, f32[12,64,128]{2,1,0:T(8,128)}, f32[54,32,64]{2,1,0:T(8,128)}, f32[18,32,64]{2,1,0:T(8,128)}, f32[24,64]{1,0:T(8,1...) custom-call(f32[24,64,128]{2,1,0:T(8,128)S(1)} %get-tuple-element.36, ...), custom_call_target="tpu_custom_call" | custom-call | tf_op jit(solution)/shard_map/deliver/pallas_call | solution.py:623

commit v6 on v5

--- a/solution.py
+++ b/solution.py
@@ -57,7 +57,7 @@
            sum_b, sum_in, sum_a, sum_o, near_b, near_in, both_b, both_in, full_b, full_in, rlane, acc_t, comp_b, tab, rtab, rsub, wtab, vtab,
            mod_b, mod_in, mod_a, mod_o, mod_w, scal, dat_b, dat_in, dat_a, dat_o, got_b, got_in, got_a, got_o, got_w, got_s,
            raw_a, raw_o, graw_a, graw_o, wcol, krow,
-           load_sem, w_sem, small_sem, first_sem, snd, rcv, psnd, prcv, bsnd, brcv, dsnd, drcv, msnd, mrcv, ssnd, srcv):
+           load_sem, w_sem, small_sem, first_sem, meet, snd, rcv, psnd, prcv, bsnd, brcv, dsnd, drcv, msnd, mrcv, ssnd, srcv):
     me = lax.axis_index('data')
     mod = lax.axis_index('model')
     n_chips = n_data // 2
@@ -105,9 +105,18 @@
             if axis != 'chip' or d % side == 0:
                 yield lax.rem(high + d // side, rows) * side + lax.rem(low + d % side, side)
 
-    for axis in ('model', 'data'):
-        for who in others(axis):
-            pl.semaphore_signal(barrier, inc=1, device_id={axis: who}, device_id_type=pl.DeviceIdType.MESH)
+    side = 4
+    z, y = lax.div(mod, side), lax.rem(mod, side)
+    neighbours = [('data', who) for who in (partner, right, left)]
+    for step in (1, side - 1):
+        neighbours.append(('model', side * z + lax.rem(y + step, side)))
+        neighbours.append(('model', side * lax.rem(z + step, n_model // side) + y))
+
+    def greet(sem):
+        for axis, who in neighbours:
+            pl.semaphore_signal(sem, inc=1, device_id={axis: who}, device_id_type=pl.DeviceIdType.MESH)
+
+    greet(barrier)
 
     def remote(src, dst, ssem, rsem, axis, who):
         return pltpu.make_async_remote_copy(src_ref=src, dst_ref=dst, send_sem=ssem, recv_sem=rsem,
@@ -521,14 +530,23 @@
     convert(0)
     for cp in small + w_loads:
         cp.start()
-    pl.semaphore_wait(barrier, n_data - 1 + n_model - 1)
+    pl.semaphore_wait(barrier, len(neighbours))
     first_pairs()
+    greet(meet.at[0])
     last = N_CH - 1 + LAG_FINISH
     steps = {}
 
     def at(k, do, *args):
         steps.setdefault(k, []).append((do, args))
 
+    def pass_on(i):
+        pl.semaphore_wait(meet.at[i], len(neighbours))
+        if i < 2:
+            greet(meet.at[i + 1])
+
+    at(2, pass_on, 0)
+    at(3, pass_on, 1)
+    at(4, pass_on, 2)
     at(4, weights_start)
     at(6, weights_next)
     at(8, weights_done)
@@ -601,6 +619,7 @@
         vmem(n_model, 2, LANES), vmem(5, n_data, 2, LANES),
         vmem(N_OUT_A, LANES), vmem(N_OUT_B, LANES), vmem(n_data, N_OUT_A, LANES), vmem(n_data, N_OUT_B, LANES), vmem(LANES, LANES), vmem(12, LANES),
         pltpu.SemaphoreType.DMA((5,)), pltpu.SemaphoreType.DMA((4,)), pltpu.SemaphoreType.DMA((8,)), pltpu.SemaphoreType.DMA((1,)),
+        pltpu.SemaphoreType.REGULAR((3,)),
         pltpu.SemaphoreType.DMA((4,)), pltpu.SemaphoreType.DMA((3, N_CH)),
         *(pltpu.SemaphoreType.DMA((n,)) for n in (2, 2, 2, 2, 4, 4, 5, 5, 5, 5)),
     ]

time: 84 us -> 83.4 us (level)
  no operation moved by 1% of the time
where the time goes in v6:
time: 83.4 us; the launch traced here: 83.3 us
  Pallas kernels  82.6 us (99%)
    pallas_call x1, Pallas kernels, step_all(): pl.pallas_call(functools.partial(kernel, n_data, n_model), name='adafacto...  81.1 us

profile of v6, /device:TPU:1, one launch (start us, length us, event | category | flops | bytes accessed | tf_op | source)
XLA Modules:
  0.0 83.3 jit_solution(879599603056930067)
XLA Ops:
  0.7 81.1 %adafactor_step.1 = (f32[24,64,128]{2,1,0:T(8,128)S(1)}, f32[12,64,128]{2,1,0:T(8,128)S(1)}, f32[54,32,64]{2,1,0:T(8,128)S(1)}, f32[18,32,64]{2,1,0:T(8,128)S(1)...) custom-call(bf16[24,512,128]{2,1,0:T(8,128)(2,1)} %bitcast.12, ...), custom_call_target="tpu_custom_call" | custom-call | tf_op jit(solution)/shard_map/adafactor_step/pallas_call | solution.py:630
  81.7 1.5 %deliver.1 = (f32[24,64,128]{2,1,0:T(8,128)}, f32[12,64,128]{2,1,0:T(8,128)}, f32[54,32,64]{2,1,0:T(8,128)}, f32[18,32,64]{2,1,0:T(8,128)}, f32[24,64]{1,0:T(8,1...) custom-call(f32[24,64,128]{2,1,0:T(8,128)S(1)} %get-tuple-element.36, ...), custom_call_target="tpu_custom_call" | custom-call | tf_op jit(solution)/shard_map/deliver/pallas_call | solution.py:642

commit v7 on v6

--- a/solution.py
+++ b/solution.py
@@ -56,7 +56,7 @@
            gin, gout, gb, part, peer, opp_in, left_in, right_in, grad, w_all, ht,
            sum_b, sum_in, sum_a, sum_o, near_b, near_in, both_b, both_in, full_b, full_in, rlane, acc_t, comp_b, tab, rtab, rsub, wtab, vtab,
            mod_b, mod_in, mod_a, mod_o, mod_w, scal, dat_b, dat_in, dat_a, dat_o, got_b, got_in, got_a, got_o, got_w, got_s,
-           raw_a, raw_o, graw_a, graw_o, wcol, krow,
+           pair_mom, raw_o, graw_o, wcol, krow,
            load_sem, w_sem, small_sem, first_sem, meet, snd, rcv, psnd, prcv, bsnd, brcv, dsnd, drcv, msnd, mrcv, ssnd, srcv):
     me = lax.axis_index('data')
     mod = lax.axis_index('model')
@@ -71,8 +71,6 @@
     whole = {'b': full_b, 'in': full_in}
     dat_got = {'b': dat_b, 'in': dat_in, 'out_a': dat_a, 'out_b': dat_o}
     mod_blk = {'b': mod_b, 'in': mod_in, 'out_a': mod_a, 'out_b': mod_o}
-    raw = {'out_a': raw_a, 'out_b': raw_o}
-    raw_got = {'out_a': graw_a, 'out_b': graw_o}
     mod_got = {'b': got_b, 'in': got_in, 'out_a': got_a, 'out_b': got_o}
 
     loads = [pltpu.make_async_copy(gq_h.at[pl.ds(0, 8)], gb.at[pl.ds(0, 8)], load_sem.at[0]),
@@ -87,8 +85,7 @@
     small = [pltpu.make_async_copy(src, dst, small_sem.at[i]) for i, (src, dst) in enumerate((
         (row_in_h, row_in), (col_in_h, col_in), (row_out_h, row_out), (col_out_h, col_out),
         (row_q_h, row_q), (col_q_h, col_q), (row_o_h, row_o), (col_o_h, col_o)))]
-    for cp in loads:
-        cp.start()
+    loads[0].start()
 
     barrier = pltpu.get_barrier_semaphore()
 
@@ -117,6 +114,8 @@
             pl.semaphore_signal(sem, inc=1, device_id={axis: who}, device_id_type=pl.DeviceIdType.MESH)
 
     greet(barrier)
+    for cp in loads[1:]:
+        cp.start()
 
     def remote(src, dst, ssem, rsem, axis, who):
         return pltpu.make_async_remote_copy(src_ref=src, dst_ref=dst, send_sem=ssem, recv_sem=rsem,
@@ -226,6 +225,9 @@
 
     lane_iota = lax.broadcasted_iota(jnp.int32, (ROWS, LANES), 1)
 
+    def row_sums(first, second):
+        return jnp.sum(jnp.concatenate([first, second], axis=0).T, axis=0, keepdims=True)
+
     def finish(ch):
         group, b0, n = CHUNKS[ch]
         family, g0, _ = GROUPS[group]
@@ -254,6 +256,10 @@
                 comp_b[pl.ds(b - FIRST_B, 1), :, 0:ROWS] = jnp.sum(st, axis=1)[None]
                 return carry
             lax.fori_loop(0, n, body, 0, unroll=2)
+        elif group == 'out_b':
+            first, second = (block(b0 + i)[1] for i in range(N_OUT_B))
+            lane_start(group)
+            mod_o[0:1, :] = row_sums(first, second)
         else:
             which = 0 if family == 'in' else 1
 
@@ -320,7 +326,7 @@
 
     def scal_ex(name, op):
         i = SLOT[name]
-        src, dst = (raw[name], raw_got[name]) if name in raw else (scal.at[i], got_s.at[i])
+        src, dst = (raw_o, graw_o) if name == 'out_b' else (scal.at[i], got_s.at[i])
         gather(src, dst, s_sems, i, 'data', op)
 
     def weights_start():
@@ -429,13 +435,8 @@
             term = jnp.where(lax.broadcasted_iota(jnp.int32, new.shape, 0) < N_QKV, new, mean_part)
         r0 = TAB_ROW[group]
         r1 = r0 + new.shape[0]
-        if family == 'out':
-            raw[group][:, 0:ROWS] = z / new
-            raw[group][:, ROWS:LANES] = term
-            scal_ex(group, 'start')
-        else:
-            tab[r0:r1, 0:ROWS] = z / new
-            tab[r0:r1, ROWS:LANES] = term
+        tab[r0:r1, 0:ROWS] = z / new
+        tab[r0:r1, ROWS:LANES] = term
         rtab[r0:r1, 0:ROWS] = lax.rsqrt(new)
         if family == 'b':
             row_q_o[...] = new[:N_QKV]
@@ -449,7 +450,7 @@
         scal[e, 0:1, :] = jnp.sum(turned[:ROWS], axis=0, keepdims=True)
         scal[e, 1:2, :] = jnp.sum(turned[ROWS:], axis=0, keepdims=True)
         scal_ex(family, 'start')
-        if family != 'b':
+        if family == 'in':
             rsub[...] = rtab[:, 0:ROWS].T
 
     def factor(q, s, w, v, family):
@@ -491,15 +492,54 @@
 
     def apply_out(group):
         _, g0, n = GROUPS[group]
-        lo, r0 = g0 - FIRST_OUT, TAB_ROW[group]
+        lo, r0, e = g0 - FIRST_OUT, TAB_ROW[group], SLOT[group]
         scal_ex(group, 'recv')
-        tot = total(raw_got[group], n_data)
-        q = jnp.sum(tot[:, 0:ROWS], axis=1, keepdims=True)
-        s = jnp.sum(tot[:, ROWS:LANES], axis=1, keepdims=True)
+        tot = total(got_s.at[e], n_data)
+        scale = factor(tot[0:1], tot[1:2], w_all[0:1, :], w_all[1:2, :], 'out')
+        krow[...] = jnp.broadcast_to(scale, (LANES, LANES)).T
+        for b in range(lo, lo + n):
+            w_out[b] = w_out[b] - grad[FIRST_OUT + b] * krow[r0 + b - lo:r0 + b - lo + 1, :]
+
+    def last_lanes():
+        _, g0, n = GROUPS['out_b']
+        lo = g0 - FIRST_OUT
+        lane_ex('out_b', 'recv')
+        new = BETA_TWO * row_out[lo:lo + n, :] + GAIN * (total(dat_o, n_data) / 512.0)
+        r = lax.rsqrt(new)
+        first, second = grad[g0] * r[0:1], grad[g0 + 1] * r[1:2]
+        mod_o[1:2, :] = row_sums(first * first, second * second)
+        model_ex('out_b', 'start')
+        grad[g0], grad[g0 + 1] = first, second
+        row_out_o[lo:lo + n, :] = new
+        pair_mom[0:1, 0:ROWS] = col_out[lo:lo + 1, :]
+        pair_mom[0:1, ROWS:LANES] = col_out[lo + 1:lo + 2, :]
+
+    def last_model():
+        lo, r0 = GROUPS['out_b'][1] - FIRST_OUT, TAB_ROW['out_b']
+        model_ex('out_b', 'recv')
+        sums_z = total(got_o, n_model)
+        sums, z = sums_z[0:1], sums_z[1:2]
+        new = BETA_TWO * pair_mom[...] + GAIN * (sums / full['out'])
+        raw_o[0:1, :] = z / new
+        raw_o[1:2, :] = GAIN * (sums / 512.0)
+        scal_ex('out_b', 'start')
+        root = lax.rsqrt(new)
+        for i in range(N_OUT_B):
+            own_lanes = slice(ROWS * i, ROWS * i + ROWS)
+            rtab[r0 + i:r0 + i + 1, 0:ROWS] = root[:, own_lanes]
+            col_out_o[lo + i:lo + i + 1, :] = new[:, own_lanes]
+
+    def last_apply():
+        _, g0, n = GROUPS['out_b']
+        lo, r0 = g0 - FIRST_OUT, TAB_ROW['out_b']
+        mine = lax.div(lax.broadcasted_iota(jnp.int32, (n, LANES), 1), ROWS) == lax.broadcasted_iota(jnp.int32, (n, LANES), 0)
+        scal_ex('out_b', 'recv')
+        tot = total(graw_o, n_data)
+        q = jnp.sum(jnp.where(mine, tot[0:1], 0.0), axis=1, keepdims=True)
+        s = jnp.sum(jnp.where(mine, tot[1:2], 0.0), axis=1, keepdims=True)
         scale = factor(q, s, wcol[r0:r0 + n, 0:1], wcol[r0:r0 + n, 1:2], 'out')
-        krow[lo:lo + n, :] = jnp.broadcast_to(scale, (n, LANES))
-        for b in range(lo, lo + n):
-            w_out[b] = w_out[b] - grad[FIRST_OUT + b] * krow[b:b + 1, :]
+        for i in range(n):
+            w_out[lo + i] = w_out[lo + i] - grad[g0 + i] * scale[i:i + 1]
 
     def sent_early():
         for i, ref in enumerate((peer, opp_in, left_in, right_in)):
@@ -558,9 +598,9 @@
     at(k_b + 6, scalars_start, 'b')
     at(k_in + 1, lane_pair, 'in')
     at(k_in + 3, lane_back, 'in')
-    tail = ((after_lanes, 'in'), (after_lanes, 'out_a'), (after_lanes, 'out_b'), (after_scalars, 'b'), (sent_early,), (after_model, 'in'),
-            (scalars_start, 'in'), (after_model, 'out_a'), (after_model, 'out_b'), (prepare_out,), (sent_mid,), (after_scalars, 'in'),
-            (apply_out, 'out_a'), (apply_out, 'out_b'), (sent_late,))
+    tail = ((after_lanes, 'in'), (after_lanes, 'out_a'), (last_lanes,), (after_scalars, 'b'), (sent_early,), (after_model, 'in'),
+            (scalars_start, 'in'), (after_model, 'out_a'), (scalars_start, 'out_a'), (last_model,), (prepare_out,), (sent_mid,), (after_scalars, 'in'),
+            (apply_out, 'out_a'), (last_apply,), (sent_late,))
     for k in range(1 - AHEAD, last + 1):
         if 0 <= k < N_CH:
             opposite(k)
@@ -575,7 +615,7 @@
         if 0 <= k - LAG_FINISH < N_CH:
             finish(k - LAG_FINISH)
         for group in GROUPS:
-            if k == LAST_CHUNK[group] + LAG_FINISH:
+            if k == LAST_CHUNK[group] + LAG_FINISH and group != 'out_b':
                 lane_start(group)
     for do, *args in tail:
         do(*args)
@@ -617,7 +657,7 @@
         vmem(n_chips, 9, LANES), vmem(n_chips, 12, LANES), vmem(n_data, N_OUT_A, LANES), vmem(n_data, N_OUT_B, LANES),
         vmem(n_model, 72, LANES), vmem(n_model, 24, LANES), vmem(n_model, N_OUT_A, LANES), vmem(n_model, N_OUT_B, LANES),
         vmem(n_model, 2, LANES), vmem(5, n_data, 2, LANES),
-        vmem(N_OUT_A, LANES), vmem(N_OUT_B, LANES), vmem(n_data, N_OUT_A, LANES), vmem(n_data, N_OUT_B, LANES), vmem(LANES, LANES), vmem(12, LANES),
+        vmem(1, LANES), vmem(N_OUT_B, LANES), vmem(n_data, N_OUT_B, LANES), vmem(LANES, LANES), vmem(LANES, LANES),
         pltpu.SemaphoreType.DMA((5,)), pltpu.SemaphoreType.DMA((4,)), pltpu.SemaphoreType.DMA((8,)), pltpu.SemaphoreType.DMA((1,)),
         pltpu.SemaphoreType.REGULAR((3,)),
         pltpu.SemaphoreType.DMA((4,)), pltpu.SemaphoreType.DMA((3, N_CH)),

time: 83.4 us -> 83.2 us (level)
  no operation moved by 1% of the time
where the time goes in v7:
time: 83.2 us; the launch traced here: 83.1 us
  Pallas kernels  82.5 us (99%)
    pallas_call x1, Pallas kernels, step_all(): pl.pallas_call(functools.partial(kernel, n_data, n_model), name='adafacto...  80.9 us

profile of v7, /device:TPU:1, one launch (start us, length us, event | category | flops | bytes accessed | tf_op | source)
XLA Modules:
  0.0 83.1 jit_solution(14161070263869448420)
XLA Ops:
  0.7 80.9 %adafactor_step.1 = (f32[24,64,128]{2,1,0:T(8,128)S(1)}, f32[12,64,128]{2,1,0:T(8,128)S(1)}, f32[54,32,64]{2,1,0:T(8,128)S(1)}, f32[18,32,64]{2,1,0:T(8,128)S(1)...) custom-call(bf16[24,512,128]{2,1,0:T(8,128)(2,1)} %bitcast.12, ...), custom_call_target="tpu_custom_call" | custom-call | tf_op jit(solution)/shard_map/adafactor_step/pallas_call | solution.py:670
  81.6 1.5 %deliver.1 = (f32[24,64,128]{2,1,0:T(8,128)}, f32[12,64,128]{2,1,0:T(8,128)}, f32[54,32,64]{2,1,0:T(8,128)}, f32[18,32,64]{2,1,0:T(8,128)}, f32[24,64]{1,0:T(8,1...) custom-call(f32[24,64,128]{2,1,0:T(8,128)S(1)} %get-tuple-element.36, ...), custom_call_target="tpu_custom_call" | custom-call | tf_op jit(solution)/shard_map/deliver/pallas_call | solution.py:682

commit v8 on v7

--- a/solution.py
+++ b/solution.py
@@ -20,9 +20,10 @@
 N_SUP = N_IN + N_B + N_OUT
 FIRST_B, FIRST_IN, FIRST_OUT = 0, N_B, N_B + N_IN
 N_QKV, N_O = 54, 18
+N_MAT = N_QKV + N_O
 N_OUT_B = 2
 N_OUT_A = N_OUT - N_OUT_B
-ROW_IN, ROW_OUT, ROW_B = 0, 24, 40
+ROW_IN, ROW_OUT, ROW_B = 0, N_IN, 40
 GROUPS = {'b': ('b', FIRST_B, N_B), 'in': ('in', FIRST_IN, N_IN), 'out_a': ('out', FIRST_OUT, N_OUT_A), 'out_b': ('out', FIRST_OUT + N_OUT_A, N_OUT_B)}
 SIZES = (('b', (2, 4, 6, 6)), ('in', (6, 6, 6, 6)), ('out_a', (4, 4, 2)), ('out_b', (2,)))
 
@@ -44,9 +45,13 @@
 OPP, LAST = 1, 2
 RECV = (D2D, OPP, OPP, LAST, LAST, LAST, LAST)
 SLOT = {'b': 0, 'in': 1, 'out_a': 2, 'out_b': 3, 'w': 4}
-LANE_ROW = {'b': 0, 'in': 24, 'out_a': 48, 'out_b': 48 + N_OUT_A}
+LANE_ROW = {'b': 0, 'in': N_IN, 'out_a': 48, 'out_b': 48 + N_OUT_A}
 TAB_ROW = {'b': ROW_B, 'in': ROW_IN, 'out_a': ROW_OUT, 'out_b': ROW_OUT + N_OUT_A}
 AHEAD, EARLY_OWN, LAG_MERGE, LAG_FINISH = 2, 3, 2, 3
+
+
+def loop(n, body, unroll):
+    lax.fori_loop(0, n, body, 0, unroll=unroll)
 
 
 def kernel(n_data, n_model, gin_h, gout_h, gq_h, go_h, win_h, wout_h, wq_h, wo_h,
@@ -75,7 +80,7 @@
 
     loads = [pltpu.make_async_copy(gq_h.at[pl.ds(0, 8)], gb.at[pl.ds(0, 8)], load_sem.at[0]),
              pltpu.make_async_copy(gq_h.at[pl.ds(8, 46)], gb.at[pl.ds(8, 46)], load_sem.at[1]),
-             pltpu.make_async_copy(go_h, gb.at[pl.ds(54, 18)], load_sem.at[2]),
+             pltpu.make_async_copy(go_h, gb.at[pl.ds(N_QKV, N_O)], load_sem.at[2]),
              pltpu.make_async_copy(gin_h, gin, load_sem.at[3]),
              pltpu.make_async_copy(gout_h, gout, load_sem.at[4])]
     w_loads = [pltpu.make_async_copy(win_h, w_in, w_sem.at[0]),
@@ -181,7 +186,7 @@
             b = b0 + i
             part[c, dest, b] = part[c, dest, b] + peer[dest, b]
             return carry
-        lax.fori_loop(0, n, body, 0, unroll=2)
+        loop(n, body, 2)
 
     def opposite(ch):
         if ch == 0:
@@ -253,13 +258,13 @@
                 g, _ = block(b)
                 gt = g.T
                 st = (gt * gt + EPS_SQ).reshape(4, WIDE, ROWS)
-                comp_b[pl.ds(b - FIRST_B, 1), :, 0:ROWS] = jnp.sum(st, axis=1)[None]
+                comp_b[pl.ds(b - FIRST_B, 1), :, :ROWS] = jnp.sum(st, axis=1)[None]
                 return carry
-            lax.fori_loop(0, n, body, 0, unroll=2)
+            loop(n, body, 2)
         elif group == 'out_b':
             first, second = (block(b0 + i)[1] for i in range(N_OUT_B))
             lane_start(group)
-            mod_o[0:1, :] = row_sums(first, second)
+            mod_o[:1, :] = row_sums(first, second)
         else:
             which = 0 if family == 'in' else 1
 
@@ -333,9 +338,9 @@
         for cp in w_loads + small:
             cp.wait()
         turn[...] = jnp.zeros_like(turn)
-        turn[0:WIDE, 0:N_QKV] = col_q[...]
+        turn[:WIDE, :N_QKV] = col_q[...]
         turn[...] = turn[...].T
-        turn[N_QKV:N_QKV + N_O, 0:WIDE] = row_o[...]
+        turn[N_QKV:N_QKV + N_O, :WIDE] = row_o[...]
         row = turn[pl.ds(0, N_B, stride=4), :]
         for q in range(1, 4):
             row = row + pltpu.roll(turn[pl.ds(q, N_B, stride=4), :], WIDE * q, 1)
@@ -348,15 +353,15 @@
                 w = ref[b]
                 wtab[pl.ds(row + b, 1), 0:width] = jnp.sum(w * w, axis=0, keepdims=True)
                 return carry
-            lax.fori_loop(0, ref.shape[0], body, 0, unroll=6)
+            loop(ref.shape[0], body, 6)
 
         squares(w_in, ROW_IN, LANES)
         squares(w_out, ROW_OUT, LANES)
         squares(w_q, ROW_B, ROWS)
         squares(w_o, ROW_B + N_QKV, ROWS)
         vtab[ROW_OUT:ROW_OUT + N_OUT, :] = row_out[...]
-        vtab[ROW_B + 54:ROW_B + 72, 0:WIDE] = row_o[...]
-        mod_w[0:1, :] = jnp.sum(wtab[...].T, axis=0, keepdims=True)
+        vtab[ROW_B + N_QKV:ROW_B + N_MAT, :WIDE] = row_o[...]
+        mod_w[:1, :] = jnp.sum(wtab[...].T, axis=0, keepdims=True)
         mod_w[1:2, :] = jnp.sum(vtab[...].T, axis=0, keepdims=True) / n_data
         gather(mod_w, got_w, m_sems, SLOT['w'], 'model', 'start')
 
@@ -368,7 +373,7 @@
     def weights_done():
         scal_ex('w', 'recv')
         w_all[...] = total(got_s.at[SLOT['w']], n_data)
-        turn[0:2, :] = w_all[...]
+        turn[:2, :] = w_all[...]
         wcol[...] = turn[...].T
 
     def after_lanes(group):
@@ -394,7 +399,7 @@
                 ht[pl.ds(4 * s, 4)] = t
                 comp_b[pl.ds(s, 1), :, ROWS:LANES] = jnp.sum(t * t, axis=1)[None]
                 return carry
-            lax.fori_loop(0, n, body, 0, unroll=3)
+            loop(n, body, 3)
             mod_b[...] = comp_b[...].reshape(4 * N_B, LANES)
         else:
             def body(b, acc):
@@ -409,9 +414,9 @@
             turn[...] = jnp.zeros_like(turn)
             for q in range(4):
                 turn[pl.ds(q, N_B, stride=4), :] = pltpu.roll(new, (LANES - WIDE * q) % LANES, 1)
-            row_o_o[...] = turn[N_QKV:N_QKV + N_O, 0:WIDE]
+            row_o_o[...] = turn[N_QKV:N_QKV + N_O, :WIDE]
             turn[...] = turn[...].T
-            col_q_o[...] = turn[0:WIDE, 0:N_QKV]
+            col_q_o[...] = turn[:WIDE, :N_QKV]
         else:
             (col_in_o if family == 'in' else row_out_o)[lo:lo + n, :] = new
 
@@ -420,7 +425,7 @@
         lo = g0 - (FIRST_OUT if family == 'out' else g0)
         model_ex(group, 'recv')
         sums_z = total(mod_got[group], n_model)
-        sums, z = sums_z[:, 0:ROWS], sums_z[:, ROWS:LANES]
+        sums, z = sums_z[:, :ROWS], sums_z[:, ROWS:LANES]
         if family == 'b':
             mom = jnp.concatenate([row_q[...], col_o[...]], axis=0)
         else:
@@ -435,9 +440,9 @@
             term = jnp.where(lax.broadcasted_iota(jnp.int32, new.shape, 0) < N_QKV, new, mean_part)
         r0 = TAB_ROW[group]
         r1 = r0 + new.shape[0]
-        tab[r0:r1, 0:ROWS] = z / new
+        tab[r0:r1, :ROWS] = z / new
         tab[r0:r1, ROWS:LANES] = term
-        rtab[r0:r1, 0:ROWS] = lax.rsqrt(new)
+        rtab[r0:r1, :ROWS] = lax.rsqrt(new)
         if family == 'b':
             row_q_o[...] = new[:N_QKV]
             col_o_o[...] = new[N_QKV:]
@@ -447,11 +452,11 @@
     def scalars_start(family):
         e = SLOT[family]
         turned = tab[...].T
-        scal[e, 0:1, :] = jnp.sum(turned[:ROWS], axis=0, keepdims=True)
+        scal[e, :1, :] = jnp.sum(turned[:ROWS], axis=0, keepdims=True)
         scal[e, 1:2, :] = jnp.sum(turned[ROWS:], axis=0, keepdims=True)
         scal_ex(family, 'start')
         if family == 'in':
-            rsub[...] = rtab[:, 0:ROWS].T
+            rsub[...] = rtab[:, :ROWS].T
 
     def factor(q, s, w, v, family):
         rows = 512.0 if family == 'in' else float(full[family])
@@ -463,15 +468,15 @@
         e = SLOT[family]
         scal_ex(family, 'recv')
         tot = total(got_s.at[e], n_data)
-        scale = factor(tot[0:1], tot[1:2], w_all[0:1, :], w_all[1:2, :], family)
+        scale = factor(tot[:1], tot[1:2], w_all[:1, :], w_all[1:2, :], family)
         if family == 'b':
             turn[...] = jnp.broadcast_to(scale, (LANES, LANES)).T
-            rtab[ROW_B:ROW_B + 72, 0:ROWS] = rtab[ROW_B:ROW_B + 72, 0:ROWS] * turn[ROW_B:ROW_B + 72, 0:ROWS]
+            rtab[ROW_B:ROW_B + N_MAT, :ROWS] = rtab[ROW_B:ROW_B + N_MAT, :ROWS] * turn[ROW_B:ROW_B + N_MAT, :ROWS]
             for ref, b0 in ((w_q, 0), (w_o, N_QKV)):
                 def body(b, carry, ref=ref, b0=b0):
-                    ref[b] = ref[b] - ht[b0 + b] * rtab[pl.ds(ROW_B + b0 + b, 1), 0:ROWS]
+                    ref[b] = ref[b] - ht[b0 + b] * rtab[pl.ds(ROW_B + b0 + b, 1), :ROWS]
                     return carry
-                lax.fori_loop(0, ref.shape[0], body, 0, unroll=6)
+                loop(ref.shape[0], body, 6)
         else:
             fac = rsub[...] * scale
 
@@ -479,23 +484,23 @@
                 f = jnp.sum(jnp.where(lane_iota == ROW_IN + b, fac, 0.0), axis=1, keepdims=True)
                 w_in[b] = w_in[b] - grad[FIRST_IN + b] * f
                 return carry
-            lax.fori_loop(0, N_IN, body, 0, unroll=4)
+            loop(N_IN, body, 4)
 
     def prepare_out():
-        fac = rtab[:, 0:ROWS].T
+        fac = rtab[:, :ROWS].T
 
         def body(b, carry):
             f = jnp.sum(jnp.where(lane_iota == ROW_OUT + b, fac, 0.0), axis=1, keepdims=True)
             grad[FIRST_OUT + b] = grad[FIRST_OUT + b] * f
             return carry
-        lax.fori_loop(0, N_OUT, body, 0, unroll=4)
+        loop(N_OUT, body, 4)
 
     def apply_out(group):
         _, g0, n = GROUPS[group]
         lo, r0, e = g0 - FIRST_OUT, TAB_ROW[group], SLOT[group]
         scal_ex(group, 'recv')
         tot = total(got_s.at[e], n_data)
-        scale = factor(tot[0:1], tot[1:2], w_all[0:1, :], w_all[1:2, :], 'out')
+        scale = factor(tot[:1], tot[1:2], w_all[:1, :], w_all[1:2, :], 'out')
         krow[...] = jnp.broadcast_to(scale, (LANES, LANES)).T
         for b in range(lo, lo + n):
             w_out[b] = w_out[b] - grad[FIRST_OUT + b] * krow[r0 + b - lo:r0 + b - lo + 1, :]
@@ -506,27 +511,27 @@
         lane_ex('out_b', 'recv')
         new = BETA_TWO * row_out[lo:lo + n, :] + GAIN * (total(dat_o, n_data) / 512.0)
         r = lax.rsqrt(new)
-        first, second = grad[g0] * r[0:1], grad[g0 + 1] * r[1:2]
+        first, second = grad[g0] * r[:1], grad[g0 + 1] * r[1:2]
         mod_o[1:2, :] = row_sums(first * first, second * second)
         model_ex('out_b', 'start')
         grad[g0], grad[g0 + 1] = first, second
         row_out_o[lo:lo + n, :] = new
-        pair_mom[0:1, 0:ROWS] = col_out[lo:lo + 1, :]
-        pair_mom[0:1, ROWS:LANES] = col_out[lo + 1:lo + 2, :]
+        pair_mom[:1, :ROWS] = col_out[lo:lo + 1, :]
+        pair_mom[:1, ROWS:LANES] = col_out[lo + 1:lo + 2, :]
 
     def last_model():
         lo, r0 = GROUPS['out_b'][1] - FIRST_OUT, TAB_ROW['out_b']
         model_ex('out_b', 'recv')
         sums_z = total(got_o, n_model)
-        sums, z = sums_z[0:1], sums_z[1:2]
+        sums, z = sums_z[:1], sums_z[1:2]
         new = BETA_TWO * pair_mom[...] + GAIN * (sums / full['out'])
-        raw_o[0:1, :] = z / new
+        raw_o[:1, :] = z / new
         raw_o[1:2, :] = GAIN * (sums / 512.0)
         scal_ex('out_b', 'start')
         root = lax.rsqrt(new)
         for i in range(N_OUT_B):
             own_lanes = slice(ROWS * i, ROWS * i + ROWS)
-            rtab[r0 + i:r0 + i + 1, 0:ROWS] = root[:, own_lanes]
+            rtab[r0 + i:r0 + i + 1, :ROWS] = root[:, own_lanes]
             col_out_o[lo + i:lo + i + 1, :] = new[:, own_lanes]
 
     def last_apply():
@@ -535,9 +540,9 @@
         mine = lax.div(lax.broadcasted_iota(jnp.int32, (n, LANES), 1), ROWS) == lax.broadcasted_iota(jnp.int32, (n, LANES), 0)
         scal_ex('out_b', 'recv')
         tot = total(graw_o, n_data)
-        q = jnp.sum(jnp.where(mine, tot[0:1], 0.0), axis=1, keepdims=True)
+        q = jnp.sum(jnp.where(mine, tot[:1], 0.0), axis=1, keepdims=True)
         s = jnp.sum(jnp.where(mine, tot[1:2], 0.0), axis=1, keepdims=True)
-        scale = factor(q, s, wcol[r0:r0 + n, 0:1], wcol[r0:r0 + n, 1:2], 'out')
+        scale = factor(q, s, wcol[r0:r0 + n, :1], wcol[r0:r0 + n, 1:2], 'out')
         for i in range(n):
             w_out[lo + i] = w_out[lo + i] - grad[g0 + i] * scale[i:i + 1]
 
@@ -622,7 +627,7 @@
 
 
 def deliver(*refs):
-    srcs, dsts, sem = refs[:12], refs[12:24], refs[24]
+    srcs, dsts, sem = refs[:12], refs[12:N_IN], refs[N_IN]
     copies = [pltpu.make_async_copy(src, dst, sem.at[i]) for i, (src, dst) in enumerate(zip(srcs, dsts))]
     for cp in copies:
         cp.start()
@@ -640,22 +645,22 @@
     def vmem(*dims):
         return pltpu.VMEM(dims, F32)
 
-    small = (vmem(24, ROWS), vmem(24, LANES), vmem(12, LANES), vmem(12, ROWS), vmem(54, ROWS), vmem(WIDE, 54), vmem(18, WIDE), vmem(18, ROWS))
-    results = (vmem(24, ROWS, LANES), vmem(12, ROWS, LANES), vmem(54, WIDE, ROWS), vmem(18, WIDE, ROWS), *small)
+    small = (vmem(N_IN, ROWS), vmem(N_IN, LANES), vmem(12, LANES), vmem(12, ROWS), vmem(N_QKV, ROWS), vmem(WIDE, N_QKV), vmem(N_O, WIDE), vmem(N_O, ROWS))
+    results = (vmem(N_IN, ROWS, LANES), vmem(12, ROWS, LANES), vmem(N_QKV, WIDE, ROWS), vmem(N_O, WIDE, ROWS), *small)
     scratch = [
         *small, vmem(N_B, LANES), vmem(LANES, LANES),
-        pltpu.VMEM((24, 512, LANES), jnp.bfloat16), pltpu.VMEM((12, LANES, 512), jnp.bfloat16),
-        pltpu.VMEM((72, WIDE, 512), jnp.bfloat16),
+        pltpu.VMEM((N_IN, 512, LANES), jnp.bfloat16), pltpu.VMEM((12, LANES, 512), jnp.bfloat16),
+        pltpu.VMEM((N_MAT, WIDE, 512), jnp.bfloat16),
         vmem(2, n_chips, N_SUP, ROWS, LANES), vmem(n_chips, N_SUP, ROWS, LANES),
         vmem(N_SUP, ROWS, LANES), vmem(N_SUP, ROWS, LANES), vmem(N_SUP, ROWS, LANES), vmem(N_SUP, ROWS, LANES),
-        vmem(2, LANES), vmem(72, WIDE, ROWS),
+        vmem(2, LANES), vmem(N_MAT, WIDE, ROWS),
         vmem(2, 9, LANES), vmem(2, 12, LANES), vmem(N_OUT_A, LANES), vmem(N_OUT_B, LANES),
         *(vmem(2, n, LANES) for n in (9, 12, 9, 12, 9, 12)),
         vmem(ROWS, LANES), vmem(2, ROWS, LANES), vmem(N_B, 4, LANES),
         vmem(LANES, LANES), vmem(LANES, LANES), vmem(ROWS, LANES), vmem(LANES, LANES), vmem(LANES, LANES),
-        vmem(72, LANES), vmem(24, LANES), vmem(N_OUT_A, LANES), vmem(N_OUT_B, LANES), vmem(2, LANES), vmem(5, 2, LANES),
+        vmem(N_MAT, LANES), vmem(N_IN, LANES), vmem(N_OUT_A, LANES), vmem(N_OUT_B, LANES), vmem(2, LANES), vmem(5, 2, LANES),
         vmem(n_chips, 9, LANES), vmem(n_chips, 12, LANES), vmem(n_data, N_OUT_A, LANES), vmem(n_data, N_OUT_B, LANES),
-        vmem(n_model, 72, LANES), vmem(n_model, 24, LANES), vmem(n_model, N_OUT_A, LANES), vmem(n_model, N_OUT_B, LANES),
+        vmem(n_model, N_MAT, LANES), vmem(n_model, N_IN, LANES), vmem(n_model, N_OUT_A, LANES), vmem(n_model, N_OUT_B, LANES),
         vmem(n_model, 2, LANES), vmem(5, n_data, 2, LANES),
         vmem(1, LANES), vmem(N_OUT_B, LANES), vmem(n_data, N_OUT_B, LANES), vmem(LANES, LANES), vmem(LANES, LANES),
         pltpu.SemaphoreType.DMA((5,)), pltpu.SemaphoreType.DMA((4,)), pltpu.SemaphoreType.DMA((8,)), pltpu.SemaphoreType.DMA((1,)),

time: 83.2 us -> 83.2 us (level)
  no operation moved by 1% of the time
where the time goes in v8:
time: 83.2 us; the launch traced here: 83.1 us
  Pallas kernels  82.5 us (99%)
    pallas_call x1, Pallas kernels, step_all(): pl.pallas_call(functools.partial(kernel, n_data, n_model), name='adafacto...  80.9 us

profile of v8, /device:TPU:1, one launch (start us, length us, event | category | flops | bytes accessed | tf_op | source)
XLA Modules:
  0.0 83.1 jit_solution(14161070263869448420)
XLA Ops:
  0.7 80.9 %adafactor_step.1 = (f32[24,64,128]{2,1,0:T(8,128)S(1)}, f32[12,64,128]{2,1,0:T(8,128)S(1)}, f32[54,32,64]{2,1,0:T(8,128)S(1)}, f32[18,32,64]{2,1,0:T(8,128)S(1)...) custom-call(bf16[24,512,128]{2,1,0:T(8,128)(2,1)} %bitcast.12, ...), custom_call_target="tpu_custom_call" | custom-call | tf_op jit(solution)/shard_map/adafactor_step/pallas_call | solution.py:675
  81.6 1.5 %deliver.1 = (f32[24,64,128]{2,1,0:T(8,128)}, f32[12,64,128]{2,1,0:T(8,128)}, f32[54,32,64]{2,1,0:T(8,128)}, f32[18,32,64]{2,1,0:T(8,128)}, f32[24,64]{1,0:T(8,1...) custom-call(f32[24,64,128]{2,1,0:T(8,128)S(1)} %get-tuple-element.36, ...), custom_call_target="tpu_custom_call" | custom-call | tf_op jit(solution)/shard_map/deliver/pallas_call | solution.py:687

commit v9 on v8

--- a/solution.py
+++ b/solution.py
@@ -455,8 +455,6 @@
         scal[e, :1, :] = jnp.sum(turned[:ROWS], axis=0, keepdims=True)
         scal[e, 1:2, :] = jnp.sum(turned[ROWS:], axis=0, keepdims=True)
         scal_ex(family, 'start')
-        if family == 'in':
-            rsub[...] = rtab[:, :ROWS].T
 
     def factor(q, s, w, v, family):
         rows = 512.0 if family == 'in' else float(full[family])
@@ -478,22 +476,22 @@
                     return carry
                 loop(ref.shape[0], body, 6)
         else:
-            fac = rsub[...] * scale
+            krow[...] = jnp.broadcast_to(scale, (LANES, LANES)).T
 
             def body(b, carry):
-                f = jnp.sum(jnp.where(lane_iota == ROW_IN + b, fac, 0.0), axis=1, keepdims=True)
-                w_in[b] = w_in[b] - grad[FIRST_IN + b] * f
+                w_in[b] = w_in[b] - grad[FIRST_IN + b] * krow[pl.ds(ROW_IN + b, 1), :]
                 return carry
             loop(N_IN, body, 4)
 
-    def prepare_out():
+    def prepare():
         fac = rtab[:, :ROWS].T
 
-        def body(b, carry):
-            f = jnp.sum(jnp.where(lane_iota == ROW_OUT + b, fac, 0.0), axis=1, keepdims=True)
-            grad[FIRST_OUT + b] = grad[FIRST_OUT + b] * f
-            return carry
-        loop(N_OUT, body, 4)
+        for g0, r0, n in ((FIRST_OUT, ROW_OUT, N_OUT), (FIRST_IN, ROW_IN, N_IN)):
+            def body(b, carry, g0=g0, r0=r0):
+                f = jnp.sum(jnp.where(lane_iota == r0 + b, fac, 0.0), axis=1, keepdims=True)
+                grad[g0 + b] = grad[g0 + b] * f
+                return carry
+            loop(n, body, 4)
 
     def apply_out(group):
         _, g0, n = GROUPS[group]
@@ -604,7 +602,7 @@
     at(k_in + 1, lane_pair, 'in')
     at(k_in + 3, lane_back, 'in')
     tail = ((after_lanes, 'in'), (after_lanes, 'out_a'), (last_lanes,), (after_scalars, 'b'), (sent_early,), (after_model, 'in'),
-            (scalars_start, 'in'), (after_model, 'out_a'), (scalars_start, 'out_a'), (last_model,), (prepare_out,), (sent_mid,), (after_scalars, 'in'),
+            (scalars_start, 'in'), (after_model, 'out_a'), (scalars_start, 'out_a'), (last_model,), (prepare,), (sent_mid,), (after_scalars, 'in'),
             (apply_out, 'out_a'), (last_apply,), (sent_late,))
     for k in range(1 - AHEAD, last + 1):
         if 0 <= k < N_CH:

time: 83.2 us -> 83.2 us (level)
  no operation moved by 1% of the time
where the time goes in v9:
time: 83.2 us; the launch traced here: 83.1 us
  Pallas kernels  82.5 us (99%)
    pallas_call x1, Pallas kernels, step_all(): pl.pallas_call(functools.partial(kernel, n_data, n_model), name='adafacto...  80.9 us

profile of v9, /device:TPU:1, one launch (start us, length us, event | category | flops | bytes accessed | tf_op | source)
XLA Modules:
  0.0 83.1 jit_solution(8647834491421584319)
XLA Ops:
  0.7 80.9 %adafactor_step.1 = (f32[24,64,128]{2,1,0:T(8,128)S(1)}, f32[12,64,128]{2,1,0:T(8,128)S(1)}, f32[54,32,64]{2,1,0:T(8,128)S(1)}, f32[18,32,64]{2,1,0:T(8,128)S(1)...) custom-call(bf16[24,512,128]{2,1,0:T(8,128)(2,1)} %bitcast.12, ...), custom_call_target="tpu_custom_call" | custom-call | tf_op jit(solution)/shard_map/adafactor_step/pallas_call | solution.py:673
  81.6 1.5 %deliver.1 = (f32[24,64,128]{2,1,0:T(8,128)}, f32[12,64,128]{2,1,0:T(8,128)}, f32[54,32,64]{2,1,0:T(8,128)}, f32[18,32,64]{2,1,0:T(8,128)}, f32[24,64]{1,0:T(8,1...) custom-call(f32[24,64,128]{2,1,0:T(8,128)S(1)} %get-tuple-element.36, ...), custom_call_target="tpu_custom_call" | custom-call | tf_op jit(solution)/shard_map/deliver/pallas_call | solution.py:685
